TPU v7x, 32 devices: a whole 2x2x4 slice. The times are simulated.
32 devices in a mesh: band: 4 (over z), px: 4 (over x, core), py: 2 (over y).
Axes of the slice: x: 2, y: 2, z: 4, core: 2. Of those that a mesh axis runs over, the one named last changes fastest.
Arguments:
- orbitals: bfloat16 [4, 1024, 384], P('band', ('px', 'py')), may hold values from -0.01171875 to 0.01171875
- occupations: float32 [4], P('band'), may hold values from 0.2 to 2
- stick_map: int32 [2, 1024], P(None, 'px'), may hold values from 0 to 191, as said below
- core_density: float32 [192, 192, 192], P('py', 'px'), may hold values from 0.05 to 0.5
Outputs:
- potential: float32 [192, 192, 192], P('py', 'px')
- gradient: float32 [3, 192, 192, 192], P(None, 'py', 'px')
Inputs may be any that keep to these rules, and one draw needn't show every extreme that they name: `stick_map`: columns i * 128 * 2 to (i + 1) * 128 * 2 - 1 have x index from i * 48 to (i + 1) * 48 - 1; no two columns share a grid position.
All inputs are finite; a program needn't handle non-finite values.
Results may differ from a plain program's by a relative error of at most 0.0054.
Values may be sent and summed in bfloat16 or wider, within the bound.
A program may use at most 128 MiB of HBM per device.

v0:
```python
import math

import jax
import jax.numpy as jnp
import numpy as np
from jax import lax
from jax.experimental.layout import Layout, with_layout_constraint
from jax.sharding import PartitionSpec as P

SPACING = 0.25
PBE_KAPPA = 0.804
PBE_MU = 0.2195
SLATER_COEF = 0.75 * (3.0 / math.pi) ** (1.0 / 3.0)
REDUCED_SCALE = 4.0 * (3.0 * math.pi**2) ** (2.0 / 3.0)
BF = jnp.bfloat16
F32 = jnp.float32
HIGH = lax.Precision.HIGH


def inverse_table(points):
    k = np.arange(points)
    angles = 2.0 * np.pi / points * (k[:, None] * k[None, :] % points)
    cosine, sine = np.cos(angles), np.sin(angles)
    return np.stack([np.stack([cosine, sine], 1), np.stack([-sine, cosine], 1)], 0)


def two_halves(table):
    high = table.astype(np.float32).astype(BF)
    low = (table - high.astype(np.float64)).astype(np.float32).astype(BF)
    return high, low


def dot2(spec, data, table):
    high, low = table
    first = jnp.einsum(spec, data, high, preferred_element_type=F32)
    return first + jnp.einsum(spec, data, low, preferred_element_type=F32)


def real_basis(points):
    pos = np.arange(points)
    freq = np.concatenate([np.arange(points // 2 + 1), np.arange(1, points // 2)])
    angle = 2.0 * np.pi / points * (pos[:, None] * freq[None, :] % points)
    basis = np.where(np.arange(points)[None, :] <= points // 2, np.cos(angle), np.sin(angle))
    scale = np.where((freq == 0) | (freq == points // 2), 1.0 / points, 2.0 / points)
    return basis * np.sqrt(scale), freq


def derivative_matrix(points):
    pos = np.arange(points)
    freq = np.arange(1, points // 2)
    unit = 2.0 * np.pi / (points * SPACING)
    lag = (pos[None, :] - pos[:, None]) % points
    values = np.zeros(points)
    for d in range(points):
        values[d] = np.sum(-2.0 * unit * freq * np.sin(2.0 * np.pi * (freq * d % points) / points)) / points
    return values[lag]


def exchange_part(density, hartree, grad_x, grad_y, grad_z):
    cube_root = jnp.cbrt(density)
    four_thirds = density * cube_root
    grad_square = grad_x * grad_x + grad_y * grad_y + grad_z * grad_z
    reduced = grad_square / (REDUCED_SCALE * four_thirds * four_thirds)
    denominator = 1.0 + PBE_MU * reduced / PBE_KAPPA
    enhance = 1.0 + PBE_KAPPA - PBE_KAPPA / denominator
    enhance_slope = PBE_MU / (denominator * denominator)
    return hartree - SLATER_COEF * cube_root * (
        4.0 / 3.0 * enhance - 8.0 / 3.0 * reduced * enhance_slope
    )


def partial_density(orbitals, occupations, stick_map, px_index):
    bands_here, columns_here, doubled = orbitals.shape
    points = doubled // 2
    rows_px = lax.axis_size("px")
    rows_py = lax.axis_size("py")
    xblock = points // rows_px
    zblock = points // rows_py
    inverse = inverse_table(points)
    z_table = two_halves(
        inverse.reshape(2, points, 2, rows_py, zblock).transpose(0, 1, 3, 2, 4).reshape(doubled, doubled)
    )
    columns = dot2("bsk,kw->bsw", orbitals, z_table).astype(BF)
    columns = lax.all_to_all(columns, "py", split_axis=2, concat_axis=1, tiled=True)
    sticks = columns.shape[1]
    columns = columns.reshape(bands_here, sticks, 2, zblock)
    y_hot = (stick_map[1][:, None] == jnp.arange(points, dtype=jnp.int32)[None, :]).astype(BF)
    x_local = stick_map[0] - px_index * xblock
    x_hot = x_local[:, None] == jnp.arange(xblock, dtype=jnp.int32)[None, :]
    by_y = inverse.reshape(2, points, 2, rows_px, xblock).transpose(1, 0, 3, 4, 2)
    picked = [
        jnp.einsum("sy,yipwo->sipwo", y_hot, half, preferred_element_type=F32).astype(BF)
        for half in two_halves(by_y)
    ]
    x_table = two_halves(inverse.reshape(2, rows_px, xblock, 2, points).transpose(1, 0, 2, 3, 4))
    total = None
    for band in range(bands_here):
        spread = jnp.where(x_hot[:, None, :, None], columns[band][:, :, None, :], jnp.zeros((), BF))
        plane = jnp.einsum("sipwo,sixz->pwoxz", picked[0], spread, preferred_element_type=F32)
        plane = plane + jnp.einsum("sipwo,sixz->pwoxz", picked[1], spread, preferred_element_type=F32)
        plane = plane.astype(BF)
        plane = lax.all_to_all(plane, "px", split_axis=0, concat_axis=0, tiled=True)
        values = dot2("pwoxz,poxtk->wztk", plane, x_table)
        weighted = occupations[band] * (values[:, :, 0] * values[:, :, 0] + values[:, :, 1] * values[:, :, 1])
        total = weighted if total is None else total + weighted
    return total


def gathered(field):
    field = with_layout_constraint(field.astype(BF), Layout((0, 1, 2)))
    return lax.all_gather(field, "band", axis=0, tiled=True)


def body(orbitals, occupations, stick_map, core_density):
    points = orbitals.shape[2] // 2
    rows_px = lax.axis_size("px")
    rows_py = lax.axis_size("py")
    groups = lax.axis_size("band")
    px_index = lax.axis_index("px")
    py_index = lax.axis_index("py")
    band_index = lax.axis_index("band")
    yblock = points // rows_px
    xblock = points // rows_px
    zblock = points // rows_py
    zshare = zblock // groups
    pieces = groups * rows_py
    kyblock = points // pieces

    density = partial_density(orbitals, occupations, stick_map, px_index)
    shares = density.astype(BF).reshape(yblock, groups, zshare, points).transpose(1, 0, 2, 3)
    shares = lax.all_to_all(shares, "band", split_axis=0, concat_axis=0, tiled=True)
    core = lax.dynamic_slice_in_dim(core_density, band_index * zshare, zshare, 0)
    rho = shares.astype(F32).sum(0) + core.transpose(1, 0, 2)

    basis, freq = real_basis(points)
    derive = derivative_matrix(points).astype(np.float32)
    basis32 = basis.astype(np.float32)
    data = jnp.einsum("yzx,xpk->pyzk", rho, basis32.reshape(points, rows_px, xblock), precision=HIGH)
    grad_x = jnp.einsum("yzx,xw->zyw", rho, derive, precision=HIGH)
    data, grad_x_sent = lax.optimization_barrier((data, grad_x.astype(BF)))
    every_x = gathered(grad_x_sent)
    data = lax.all_to_all(data, "px", split_axis=0, concat_axis=0, tiled=True)
    data = data.reshape(points, zshare, xblock)
    high_basis, low_basis = two_halves(basis)
    x_basis = (high_basis.reshape(points, rows_px, xblock), low_basis.reshape(points, rows_px, xblock))
    lines_y = jnp.einsum("yzk,yw->wzk", data, derive, precision=HIGH).astype(BF)
    lines_y = lines_y.reshape(rows_px, yblock, zshare, xblock)
    lines_y = lax.all_to_all(lines_y, "px", split_axis=0, concat_axis=0, tiled=True)
    grad_y = dot2("pyzk,xpk->zyx", lines_y, x_basis)
    grad_y_sent = grad_y.astype(BF)
    modes = jnp.einsum("yzk,yj->jzk", data, basis32, precision=HIGH)
    modes = modes.reshape(pieces, kyblock, zshare, xblock)
    modes = lax.all_to_all(modes, ("band", "py"), split_axis=0, concat_axis=0, tiled=True)
    source = np.arange(points)
    device, within = source // zshare, source % zshare
    z_order = device % rows_py * zblock + device // rows_py * zshare + within
    z_basis = basis32[z_order].reshape(pieces, zshare, points)
    z_derive = derive[z_order][:, z_order].reshape(pieces, zshare, pieces, zshare)
    spectrum = jnp.einsum("djzk,dzm->mjk", modes, z_basis, precision=HIGH)
    unit = 2.0 * math.pi / (points * SPACING)
    all_q = jnp.asarray((freq * freq).astype(np.float32))
    q_col = lax.dynamic_slice_in_dim(all_q, (band_index * rows_py + py_index) * kyblock, kyblock)
    q_row = lax.dynamic_slice_in_dim(all_q, px_index * xblock, xblock)
    squared = unit**2 * (all_q[:, None, None] + q_col[None, :, None] + q_row[None, None, :])
    factor = jnp.where(squared > 0, 4.0 * math.pi / jnp.where(squared > 0, squared, 1.0), 0.0)
    spectrum = spectrum * factor
    back = jnp.stack(
        [
            jnp.einsum("mjk,dzm->djzk", spectrum, z_basis, precision=HIGH).astype(BF),
            jnp.einsum("ejwk,ewdz->djzk", modes, z_derive, precision=HIGH).astype(BF),
        ],
        1,
    )
    back, every_y, every_x = lax.optimization_barrier((back, grad_y_sent, every_x))
    every_y = gathered(every_y)
    back = lax.all_to_all(back, ("band", "py"), split_axis=0, concat_axis=0, tiled=True)
    y_basis = (high_basis.reshape(points, pieces, kyblock), low_basis.reshape(points, pieces, kyblock))
    lines = dot2("dfjzk,ydj->fyzk", back, y_basis)
    lines = lines.astype(BF).reshape(2, rows_px, yblock, zshare, xblock)
    lines = lax.all_to_all(lines, "px", split_axis=1, concat_axis=1, tiled=True)
    fields = dot2("fpyzk,xpk->fzyx", lines, x_basis)
    every_z = gathered(fields[1])
    potential = exchange_part(rho.transpose(1, 0, 2), fields[0], grad_x, grad_y, fields[1])
    every_potential = gathered(potential)
    gradient = jnp.stack([every_x.astype(F32), every_y.astype(F32), every_z.astype(F32)])
    return (every_potential.astype(F32), gradient)


def solution(mesh):
    return jax.shard_map(
        body,
        mesh=mesh,
        in_specs=(P("band", ("px", "py"), None), P("band"), P(None, "px"), P("py", "px", None)),
        out_specs=(P("py", "px", None), P(None, "py", "px", None)),
        check_vma=False,
    )
```

profile of v0, /device:TPU:1, one launch (start us, length us, event | category | flops | bytes accessed | tf_op | source)
XLA Modules:
  0.0 489.7 jit_solution(10835476678596316135)
XLA Ops:
  20.5 5.3 %fusion.4 = f32[4,48,2,48,96,1]{4,1,5,3,2,0:T(8,128)} fusion(pred[256,48]{0,1:T(8,128)(4,1)S(1)} %iota_compare_fusion.1, bf16[256,2,96]{0,2,1:T(8,128)(2,1)S(1)} %broadcast_in_dim.35, bf16[192,2,4,48,2]{0,3,1,4,2:T(8,128)(2,1)S(1)} %copy-done.20, s32[256]{0:T(256)S(1)} %bitcast.243), kind=kOutput, calls=%fused_computation.9 | convolution fusion | flops 1890041856 | bytes 7484416 | tf_op jit(solution)/shard_map/sipwo,sixz->pwoxz/dot_general | solution.py:100
  25.9 6.9 %fusion = bf16[4,48,2,48,96]{4,1,3,2,0:T(8,128)(2,1)} fusion(f32[4,48,2,48,96,1]{4,1,5,3,2,0:T(8,128)} %fusion.4, pred[256,48]{0,1:T(8,128)(4,1)S(1)} %iota_compare_fusion.1, bf16[256,2,96]{0,2,1:T(8,128)(2,1)S(1)} %broadcast_in_dim.35, bf16[192,2,4,48,2]{0,3,1,4,2:T(8,128)(2,1)S(1)} %copy-done.19, s32[256]{0:T(256)S(1)} %bitcast.244), kind=kOutput, calls=%fused_computation.2 | convolution fusion | flops 1893580800 | bytes 11023360 | tf_op jit(solution)/shard_map/sipwo,sixz->pwoxz/dot_general | solution.py:99
  32.8 6.6 %all-to-all-start.1 = ((bf16[4,48,2,48,96]{4,1,3,2,0:T(8,128)(2,1)}), bf16[4,48,2,48,96]{4,1,3,2,0:T(8,128)(2,1)}, u32[]{:S(2)}, u32[]{:S(2)}) async-start(bf16[4,48,2,48,96]{4,1,3,2,0:T(8,128)(2,1)} %fusion), calls=%async_computation.1 | async-start | bytes 9437184 | tf_op jit(solution)/shard_map/all_to_all | solution.py:102
  40.0 52.2 %all-to-all-done.1 = bf16[4,48,2,48,96]{4,1,3,2,0:T(8,128)(2,1)} async-done(((bf16[4,48,2,48,96]{4,1,3,2,0:T(8,128)(2,1)}), bf16[4,48,2,48,96]{4,1,3,2,0:T(8,128)(2,1)}, u32[]{:S(2)}, u32[]{:S(2)}) %all-to-all-start.1) | async-done | bytes 3538976 | tf_op jit(solution)/shard_map/all_to_all | solution.py:102
  92.3 5.6 %fusion.12 = f32[48,96,2,192,1,1]{3,1,5,4,2,0:T(8,128)S(1)} fusion(bf16[4,2,48,2,192,1]{4,2,0,1,3,5:T(8,128)(2,1)S(1)} %copy-done.10, bf16[4,48,2,48,96,1]{4,1,3,2,0,5:T(8,128)(2,1)} %bitcast.21), kind=kOutput, calls=%fused_computation.18 | convolution fusion | flops 1358954496 | bytes 10911744 | tf_op jit(solution)/shard_map/pwoxz,poxtk->wztk/dot_general | solution.py:36
  97.9 5.6 %bitcast_add_fusion = f32[48,96,2,192]{3,1,2,0:T(8,128)S(1)} fusion(f32[48,96,2,192,1,1]{3,1,5,4,2,0:T(8,128)S(1)} %fusion.12, bf16[4,2,48,2,192,1]{4,2,0,1,3,5:T(8,128)(2,1)S(1)} %copy-done.9, bf16[4,48,2,48,96,1]{4,1,3,2,0,5:T(8,128)(2,1)} %bitcast.21), kind=kOutput, calls=%fused_computation | convolution fusion | flops 1360723968 | bytes 17989632 | tf_op jit(solution)/shard_map/pwoxz,poxtk->wztk/dot_general | solution.py:35
  106.2 5.3 %all-to-all-start.2 = ((bf16[4,48,24,192]{3,2,1,0:T(8,128)(2,1)}), bf16[4,48,24,192]{3,2,1,0:T(8,128)(2,1)S(1)}, u32[]{:S(2)}, u32[]{:S(2)}) async-start(bf16[4,48,24,192]{3,2,1,0:T(8,128)(2,1)} %bitcast.229), calls=%async_computation.2 | async-start | bytes 4718592 | tf_op jit(solution)/shard_map/all_to_all | solution.py:131
  111.5 53.4 %all-to-all-done.2 = bf16[4,48,24,192]{3,2,1,0:T(8,128)(2,1)S(1)} async-done(((bf16[4,48,24,192]{3,2,1,0:T(8,128)(2,1)}), bf16[4,48,24,192]{3,2,1,0:T(8,128)(2,1)S(1)}, u32[]{:S(2)}, u32[]{:S(2)}) %all-to-all-start.2) | async-done | bytes 1769504 | tf_op jit(solution)/shard_map/all_to_all | solution.py:131
  176.2 16.6 %all_to_all.50 = f32[4,1,55296]{2,1,0:T(1,128)S(1)} all-to-all(f32[4,1,55296]{2,1,0:T(1,128)} %reshape.140), channel_id=1, replica_groups=mesh['band'=4,'px'=4,'py'=2] {'px'}, dimensions={0} | all-to-all | bytes 1769472 | tf_op jit(solution)/shard_map/all_to_all | solution.py:142
  207.6 5.0 %all-to-all-start.5 = ((bf16[4,2,27648]{2,1,0:T(2,128)(2,1)}), bf16[4,2,27648]{2,1,0:T(2,128)(2,1)}, u32[]{:S(2)}, u32[]{:S(2)}) async-start(bf16[4,2,27648]{2,1,0:T(2,128)(2,1)} %reshape.144), calls=%async_computation.5 | async-start | bytes 884736 | tf_op jit(solution)/shard_map/all_to_all | solution.py:148
  230.5 41.1 %all-to-all-done.4 = f32[8,1,27648]{2,1,0:T(1,128)S(1)} async-done(((f32[8,1,27648]{2,1,0:T(1,128)}), f32[8,1,27648]{2,1,0:T(1,128)S(1)}, u32[]{:S(2)}, u32[]{:S(2)}) %all-to-all-start.4) | async-done | bytes 884768 | tf_op jit(solution)/shard_map/all_to_all | solution.py:153
  276.8 4.1 fusion.50
  286.5 6.6 %reshape.146 = bf16[8,2,27648]{2,1,0:T(2,128)(2,1)} reshape(bf16[8,2,24,24,48]{4,3,2,1,0:T(8,128)(2,1)} %copy.110) | data formatting | bytes 1769472
  293.1 4.2 all-to-all-start.6
  298.1 30.2 %all-to-all-done.6 = bf16[8,2,27648]{2,1,0:T(2,128)(2,1)} async-done(((bf16[8,2,27648]{2,1,0:T(2,128)(2,1)}), bf16[8,2,27648]{2,1,0:T(2,128)(2,1)}, u32[]{:S(2)}, u32[]{:S(2)}) %all-to-all-start.6) | async-done | bytes 884768 | tf_op jit(solution)/shard_map/all_to_all | solution.py:176
  328.3 3.8 reshape.147
  335.7 3.9 reshape.102
  343.2 4.8 reshape.148
  347.9 21.6 %all_to_all.51 = bf16[4,2,55296]{2,1,0:T(2,128)(2,1)} all-to-all(bf16[4,2,55296]{2,1,0:T(2,128)(2,1)S(1)} %reshape.148), channel_id=1, replica_groups=mesh['band'=4,'px'=4,'py'=2] {'px'}, dimensions={0} | all-to-all | bytes 1769472 | tf_op jit(solution)/shard_map/all_to_all | solution.py:180
  378.4 5.2 %fusion.58 = bf16[24,48,192]{2,1,0:T(8,128)(2,1)} fusion(f32[2,24,48,192]{3,2,1,0:T(8,128)} %copy-done.2, f32[48,24,192]{2,0,1:T(8,128)S(1)} %copy-done.4, f32[48,24,192]{2,0,1:T(8,128)} %copy-done.5, f32[48,24,192]{2,1,0:T(8,128)S(1)} %convert_reduce_fusion, f32[96,48,192]{2,1,0:T(8,128)} %param.27, s32[]{:T(128)S(6)} %select_n.21), kind=kLoop, calls=%fused_computation.68 | loop fusion | flops 5308416 | bytes 5750788 | tf_op jit(solution)/shard_map/convert_element_type | solution.py:110
  383.6 44.6 %all-gather.11.cloned.1.call-done = bf16[96,48,192]{2,1,0:T(8,128)(2,1)} async-done(((bf16[24,48,192]{2,1,0:T(8,128)(2,1)}), bf16[96,48,192]{2,1,0:T(8,128)(2,1)}) %all-gather.11.cloned.1.call-update) | async-done | bytes 1769488 | tf_op jit(solution)/shard_map/all_gather | solution.py:111
  428.3 10.5 %maximum_convert_fusion = f32[3,96,48,192]{3,2,1,0:T(8,128)} fusion(bf16[1,96,48,192]{3,2,1,0:T(8,128)(2,1)} %bitcast.238, bf16[1,96,48,192]{3,2,1,0:T(8,128)(2,1)} %bitcast.237, bf16[1,96,48,192]{3,2,1,0:T(8,128)(2,1)} %bitcast.236), kind=kLoop, calls=%fused_computation.3 | loop fusion | flops 7962624 | bytes 15925248 | tf_op jit(solution)/shard_map/stack | solution.py:185
  438.8 39.7 %all-gather.7.cloned.1.call-done = bf16[96,48,192]{2,1,0:T(8,128)(2,1)} async-done(((bf16[24,48,192]{2,1,0:T(8,128)(2,1)}), bf16[96,48,192]{2,1,0:T(8,128)(2,1)}) %all-gather.7.cloned.1.call-update) | async-done | bytes 1769488 | tf_op jit(solution)/shard_map/all_gather | solution.py:111
  478.5 4.5 convert_element_type.98
  (107 shorter events, 87.2 us)
Async XLA Ops:
  7.2 13.3 %copy-start.20 = (bf16[192,2,4,48,2]{0,3,1,4,2:T(8,128)(2,1)S(1)}, bf16[192,2,4,48,2]{0,3,1,4,2:T(8,128)(2,1)}, u32[]{:S(2)}) copy-start(bf16[192,2,4,48,2]{0,3,1,4,2:T(8,128)(2,1)} %constant.87.clone) | copy-start | bytes 884740
  13.1 7.1 %all-to-all-start = ((bf16[2,2,12288]{2,1,0:T(2,128)(2,1)}), bf16[2,2,12288]{2,1,0:T(2,128)(2,1)S(1)}, u32[]{:S(2)}, u32[]{:S(2)}) async-start(bf16[2,2,12288]{2,1,0:T(2,128)(2,1)} %reshape.138), calls=%async_computation | async-start | bytes 196608 | tf_op jit(solution)/shard_map/all_to_all | solution.py:84
  20.5 5.4 %copy-start.19 = (bf16[192,2,4,48,2]{0,3,1,4,2:T(8,128)(2,1)S(1)}, bf16[192,2,4,48,2]{0,3,1,4,2:T(8,128)(2,1)}, u32[]{:S(2)}) copy-start(bf16[192,2,4,48,2]{0,3,1,4,2:T(8,128)(2,1)} %constant.86.clone) | copy-start | bytes 884740
  32.8 59.5 %copy-start.10 = (bf16[4,2,48,2,192,1]{4,2,0,1,3,5:T(8,128)(2,1)S(1)}, bf16[4,2,48,2,192,1]{4,2,0,1,3,5:T(8,128)(2,1)}, u32[]{:S(2)}) copy-start(bf16[4,2,48,2,192,1]{4,2,0,1,3,5:T(8,128)(2,1)} %constant.104) | copy-start | bytes 884740
  32.8 59.5 %all-to-all-start.1 = ((bf16[4,48,2,48,96]{4,1,3,2,0:T(8,128)(2,1)}), bf16[4,48,2,48,96]{4,1,3,2,0:T(8,128)(2,1)}, u32[]{:S(2)}, u32[]{:S(2)}) async-start(bf16[4,48,2,48,96]{4,1,3,2,0:T(8,128)(2,1)} %fusion), calls=%async_computation.1 | async-start | bytes 9437184 | tf_op jit(solution)/shard_map/all_to_all | solution.py:102
  92.3 5.6 %copy-start.9 = (bf16[4,2,48,2,192,1]{4,2,0,1,3,5:T(8,128)(2,1)S(1)}, bf16[4,2,48,2,192,1]{4,2,0,1,3,5:T(8,128)(2,1)}, u32[]{:S(2)}) copy-start(bf16[4,2,48,2,192,1]{4,2,0,1,3,5:T(8,128)(2,1)} %constant.103) | copy-start | bytes 884740
  106.2 58.6 %all-to-all-start.2 = ((bf16[4,48,24,192]{3,2,1,0:T(8,128)(2,1)}), bf16[4,48,24,192]{3,2,1,0:T(8,128)(2,1)S(1)}, u32[]{:S(2)}, u32[]{:S(2)}) async-start(bf16[4,48,24,192]{3,2,1,0:T(8,128)(2,1)} %bitcast.229), calls=%async_computation.2 | async-start | bytes 4718592 | tf_op jit(solution)/shard_map/all_to_all | solution.py:131
  165.3 1.8 copy-start.7
  167.0 4.4 copy-start.11
  199.1 2.4 copy-start.8
  207.6 13.8 %all-to-all-start.5 = ((bf16[4,2,27648]{2,1,0:T(2,128)(2,1)}), bf16[4,2,27648]{2,1,0:T(2,128)(2,1)}, u32[]{:S(2)}, u32[]{:S(2)}) async-start(bf16[4,2,27648]{2,1,0:T(2,128)(2,1)} %reshape.144), calls=%async_computation.5 | async-start | bytes 884736 | tf_op jit(solution)/shard_map/all_to_all | solution.py:148
  212.6 71.9 %all-gather.5.cloned.1.call-start = ((), (), s32[]{:S(2)}) async-start(), calls=%async_computation.8 | async-start | bytes 2949120 | tf_op jit(solution)/shard_map/all_gather | solution.py:111
  218.1 7.0 %copy-start.17 = (f32[192]{0:T(256)S(1)}, f32[192]{0:T(256)}, u32[]{:S(2)}) copy-start(f32[192]{0:T(256)} %constant.96.clone) | copy-start | bytes 2308
  221.3 6.4 %copy-start.14 = (bf16[192,4,48,1]{0,2,1,3:T(8,128)(2,1)S(1)}, bf16[192,4,48,1]{0,2,1,3:T(8,128)(2,1)}, u32[]{:S(2)}) copy-start(bf16[192,4,48,1]{0,2,1,3:T(8,128)(2,1)} %constant.109) | copy-start | bytes 221188
  221.3 50.3 %all-to-all-start.4 = ((f32[8,1,27648]{2,1,0:T(1,128)}), f32[8,1,27648]{2,1,0:T(1,128)S(1)}, u32[]{:S(2)}, u32[]{:S(2)}) async-start(f32[8,1,27648]{2,1,0:T(1,128)} %reshape.142), calls=%async_computation.4 | async-start | bytes 1769472 | tf_op jit(solution)/shard_map/all_to_all | solution.py:153
  225.0 3.2 copy-start.16
  230.5 46.3 %copy-start.12 = (f32[8,24,192,1]{2,1,0,3:T(8,128)S(1)}, f32[8,24,192,1]{2,1,0,3:T(8,128)}, u32[]{:S(2)}) copy-start(f32[8,24,192,1]{2,1,0,3:T(8,128)} %constant.102) | copy-start | bytes 442372
  276.8 5.2 %copy-start.18 = (f32[8,24,8,24,1]{1,3,0,2,4:T(8,128)S(1)}, f32[8,24,8,24,1]{1,3,0,2,4:T(8,128)}, u32[]{:S(2)}) copy-start(f32[8,24,8,24,1]{1,3,0,2,4:T(8,128)} %constant.107) | copy-start | bytes 442372
  293.1 35.2 %all-to-all-start.6 = ((bf16[8,2,27648]{2,1,0:T(2,128)(2,1)}), bf16[8,2,27648]{2,1,0:T(2,128)(2,1)}, u32[]{:S(2)}, u32[]{:S(2)}) async-start(bf16[8,2,27648]{2,1,0:T(2,128)(2,1)} %reshape.146), calls=%async_computation.6 | async-start | bytes 1769472 | tf_op jit(solution)/shard_map/all_to_all | solution.py:176
  297.3 86.3 %all-gather.9.cloned.1.call-start = ((), (), s32[]{:S(2)}) async-start(), calls=%async_computation.10 | async-start | bytes 2949120 | tf_op jit(solution)/shard_map/all_gather | solution.py:111
  298.1 130.2 %all-gather.11.cloned.1.call-start = ((), (), s32[]{:S(2)}) async-start(), calls=%async_computation.11 | async-start | bytes 2949120 | tf_op jit(solution)/shard_map/all_gather | solution.py:111
  332.1 1.7 copy-start.15
  377.8 100.7 %all-gather.7.cloned.1.call-start = ((), (), s32[]{:S(2)}) async-start(), calls=%async_computation.9 | async-start | bytes 2949120 | tf_op jit(solution)/shard_map/all_gather | solution.py:111
  428.3 54.7 %copy-start.1 = (bf16[1,128,384]{2,1,0:T(8,128)(2,1)S(1)}, bf16[1,128,384]{2,1,0:T(8,128)(2,1)}, u32[]{:S(2)}) copy-start(bf16[1,128,384]{2,1,0:T(8,128)(2,1)} %param.24) | copy-start | bytes 294916
  (7 other events, 9.2 us)
Sparse Core Ops, SparseCore 0:
  214.9 66.7 all-gather.4
  299.7 58.7 all-gather.8
  377.9 50.3 all-gather.10
  429.7 48.7 all-gather.6
where the time goes:
time: 499 us; the launch traced here: 490 us
  waiting for transfers between devices  265 us (53%)
  local copies, waits for them, and re-layouts  61.4 us (12%)
  matrix products  47 us (9%)
  blocking collectives  38.2 us (8%)
  other arithmetic  33.9 us (7%)
  starting transfers between devices  28.8 us (6%)
  between operations  15.2 us (3%)
    all_gather x4, waiting for transfers between devices, gathered(): return lax.all_gather(field, 'band', axis=0, tiled=True)  84.4 us
    all_to_all x1, waiting for transfers between devices, body(): lax.all_to_all(shares, 'band', split_axis=0, concat_axis=0, tiled=True)  53.4 us
    all_to_all x1, waiting for transfers between devices, partial_density(): plane = lax.all_to_all(plane, 'px', split_axis=0, concat_axis=0, tiled=True)  52.2 us
    unnamed x56, local copies, waits for them, and re-layouts  41.8 us
    all_to_all x1, waiting for transfers between devices, body(): lax.all_to_all(modes, ('band', 'py'), split_axis=0, concat_axis=0, tiled=...  41.1 us
    all_to_all x1, waiting for transfers between devices, body(): lax.all_to_all(back, ('band', 'py'), split_axis=0, concat_axis=0, tiled=T...  30.2 us
    all_to_all x1, blocking collectives, body(): lines = lax.all_to_all(lines, 'px', split_axis=1, concat_axis=1, tiled=True)  21.6 us
    all_to_all x1, blocking collectives, body(): data = lax.all_to_all(data, 'px', split_axis=0, concat_axis=0, tiled=True)  16.6 us
  transfers between devices with their start and end apart: 10, of which 7 were waited for; matrix products, arithmetic and copies ran while one was open for 14% of the time, Pallas kernels for 0%

commit v1 on v0

--- a/solution.py
+++ b/solution.py
@@ -69,41 +69,49 @@
     )
 
 
-def partial_density(orbitals, occupations, stick_map, px_index):
+def share_density(orbitals, occupations, stick_map, px_index):
     bands_here, columns_here, doubled = orbitals.shape
     points = doubled // 2
     rows_px = lax.axis_size("px")
     rows_py = lax.axis_size("py")
+    groups = lax.axis_size("band")
     xblock = points // rows_px
-    zblock = points // rows_py
+    yblock = points // rows_px
+    pieces = groups * rows_py
+    zshare = points // pieces
+    sticks = columns_here * rows_py
+    bands = groups * bands_here
     inverse = inverse_table(points)
-    z_table = two_halves(
-        inverse.reshape(2, points, 2, rows_py, zblock).transpose(0, 1, 3, 2, 4).reshape(doubled, doubled)
-    )
-    columns = dot2("bsk,kw->bsw", orbitals, z_table).astype(BF)
-    columns = lax.all_to_all(columns, "py", split_axis=2, concat_axis=1, tiled=True)
-    sticks = columns.shape[1]
-    columns = columns.reshape(bands_here, sticks, 2, zblock)
-    y_hot = (stick_map[1][:, None] == jnp.arange(points, dtype=jnp.int32)[None, :]).astype(BF)
-    x_local = stick_map[0] - px_index * xblock
-    x_hot = x_local[:, None] == jnp.arange(xblock, dtype=jnp.int32)[None, :]
-    by_y = inverse.reshape(2, points, 2, rows_px, xblock).transpose(1, 0, 3, 4, 2)
+    z_order = inverse.reshape(2, points, 2, rows_py, groups, zshare).transpose(0, 1, 4, 3, 2, 5)
+    z_table = two_halves(z_order.reshape(doubled, pieces, 2 * zshare))
+    columns = dot2("bsk,kdw->dbsw", orbitals, z_table).astype(BF)
+    columns = lax.all_to_all(columns, ("band", "py"), split_axis=0, concat_axis=0, tiled=True)
+    columns = lax.all_gather(columns, "px", axis=0, tiled=False)
+    columns = columns.reshape(rows_px, groups, rows_py, bands_here, columns_here, 2, zshare)
+    columns = columns.transpose(0, 2, 4, 5, 1, 3, 6).reshape(rows_px, sticks, 2, bands * zshare)
+    places = lax.all_gather(stick_map, "px", axis=0, tiled=False)
+    weights = lax.all_gather(occupations, "band", axis=0, tiled=True)
+    y_hot = (places[:, 1, :, None] == jnp.arange(points, dtype=jnp.int32)).astype(BF)
+    x_local = places[:, 0] - jnp.arange(rows_px, dtype=jnp.int32)[:, None] * xblock
+    x_hot = x_local[:, :, None] == jnp.arange(xblock, dtype=jnp.int32)
+    by_y = inverse.reshape(2, points, 2, rows_px, yblock).transpose(3, 1, 0, 4, 2)
     picked = [
-        jnp.einsum("sy,yipwo->sipwo", y_hot, half, preferred_element_type=F32).astype(BF)
+        jnp.einsum(
+            "psy,yiwo->psiwo",
+            y_hot,
+            lax.dynamic_index_in_dim(jnp.asarray(half), px_index, 0, keepdims=False),
+            preferred_element_type=F32,
+        ).astype(BF)
         for half in two_halves(by_y)
     ]
     x_table = two_halves(inverse.reshape(2, rows_px, xblock, 2, points).transpose(1, 0, 2, 3, 4))
-    total = None
-    for band in range(bands_here):
-        spread = jnp.where(x_hot[:, None, :, None], columns[band][:, :, None, :], jnp.zeros((), BF))
-        plane = jnp.einsum("sipwo,sixz->pwoxz", picked[0], spread, preferred_element_type=F32)
-        plane = plane + jnp.einsum("sipwo,sixz->pwoxz", picked[1], spread, preferred_element_type=F32)
-        plane = plane.astype(BF)
-        plane = lax.all_to_all(plane, "px", split_axis=0, concat_axis=0, tiled=True)
-        values = dot2("pwoxz,poxtk->wztk", plane, x_table)
-        weighted = occupations[band] * (values[:, :, 0] * values[:, :, 0] + values[:, :, 1] * values[:, :, 1])
-        total = weighted if total is None else total + weighted
-    return total
+    spread = jnp.where(x_hot[:, :, None, :, None], columns[:, :, :, None, :], jnp.zeros((), BF))
+    plane = jnp.einsum("psiwo,psixz->pwoxz", picked[0], spread, preferred_element_type=F32)
+    plane = plane + jnp.einsum("psiwo,psixz->pwoxz", picked[1], spread, preferred_element_type=F32)
+    values = dot2("pwoxz,poxtk->wztk", plane.astype(BF), x_table)
+    values = values.reshape(yblock, bands, zshare, 2, points)
+    square = values[:, :, :, 0] * values[:, :, :, 0] + values[:, :, :, 1] * values[:, :, :, 1]
+    return (weights[None, :, None, None] * square).sum(1)
 
 
 def gathered(field):
@@ -126,11 +134,9 @@
     pieces = groups * rows_py
     kyblock = points // pieces
 
-    density = partial_density(orbitals, occupations, stick_map, px_index)
-    shares = density.astype(BF).reshape(yblock, groups, zshare, points).transpose(1, 0, 2, 3)
-    shares = lax.all_to_all(shares, "band", split_axis=0, concat_axis=0, tiled=True)
+    density = share_density(orbitals, occupations, stick_map, px_index)
     core = lax.dynamic_slice_in_dim(core_density, band_index * zshare, zshare, 0)
-    rho = shares.astype(F32).sum(0) + core.transpose(1, 0, 2)
+    rho = density + core.transpose(1, 0, 2)
 
     basis, freq = real_basis(points)
     derive = derivative_matrix(points).astype(np.float32)

time: 499 us -> 397 us (0.80)
  waiting for transfers between devices: 265 us -> 158 us
  blocking collectives: 38.2 us -> 61.2 us
  starting transfers between devices: 28.8 us -> 18.5 us
  local copies, waits for them, and re-layouts: 61.4 us -> 53.8 us
    all_to_all x3 -> x1, waiting for transfers between devices: 109 us -> 0.01 us  [share_density(): lax.all_to_all(columns, ('band', 'py'), split_axis=0, concat_axis=0, tile...]
    all_gather x0 -> x2, blocking collectives: none -> 15 us  [the longest x1 8.39 us: share_density(): places = lax.all_gather(stick_map, 'px', axis=0, tiled=False)]
    unnamed x0 -> x1, blocking collectives: none -> 9.84 us
    dot_general x2, matrix products: 12.3 us -> 21.8 us  [the longest x1 11.2 us: share_density(): jnp.einsum('psiwo,psixz->pwoxz', picked[0], spread, preferred_element_typ...]
    all_to_all x3 -> x1, starting transfers between devices: 15.2 us -> 6.37 us  [share_density(): lax.all_to_all(columns, ('band', 'py'), split_axis=0, concat_axis=0, tile...]
    unnamed x56 -> x60, local copies, waits for them, and re-layouts: 41.8 us -> 36.3 us
  transfers between devices with their start and end apart: 10 -> 8, of which waited for: 7 -> 5; matrix products, arithmetic and copies ran while one was open for 14% -> 15% of each run, Pallas kernels for 0% -> 0%
where the time goes in v1:
time: 397 us; the launch traced here: 390 us
  waiting for transfers between devices  158 us (40%)
  blocking collectives  61.2 us (15%)
  local copies, waits for them, and re-layouts  53.8 us (14%)
  matrix products  49.7 us (13%)
  other arithmetic  32.9 us (8%)
  starting transfers between devices  18.5 us (5%)
  between operations  15.1 us (4%)
    all_gather x4, waiting for transfers between devices, gathered(): return lax.all_gather(field, 'band', axis=0, tiled=True)  85.4 us
    all_to_all x1, waiting for transfers between devices, body(): lax.all_to_all(modes, ('band', 'py'), split_axis=0, concat_axis=0, tiled=...  41.7 us
    unnamed x60, local copies, waits for them, and re-layouts  36.3 us
    all_to_all x1, waiting for transfers between devices, body(): lax.all_to_all(back, ('band', 'py'), split_axis=0, concat_axis=0, tiled=T...  29.8 us
    all_to_all x1, blocking collectives, body(): lines = lax.all_to_all(lines, 'px', split_axis=1, concat_axis=1, tiled=True)  21.8 us
    all_to_all x1, blocking collectives, body(): data = lax.all_to_all(data, 'px', split_axis=0, concat_axis=0, tiled=True)  14.6 us
    dot_general x1, matrix products, share_density(): jnp.einsum('psiwo,psixz->pwoxz', picked[0], spread, preferred_element_typ...  11.2 us
    dot_general x1, matrix products, share_density(): jnp.einsum('psiwo,psixz->pwoxz', picked[1], spread, preferred_element_typ...  10.5 us
  transfers between devices with their start and end apart: 8, of which 5 were waited for; matrix products, arithmetic and copies ran while one was open for 15% of the time, Pallas kernels for 0%

profile of v1, /device:TPU:1, one launch (start us, length us, event | category | flops | bytes accessed | tf_op | source)
XLA Modules:
  0.0 389.6 jit_solution(4171012105546655619)
XLA Ops:
  11.2 6.4 %all-to-all-start = ((bf16[8,1,128,48]{2,3,1,0:T(8,128)(2,1)}), bf16[8,1,128,48]{2,3,1,0:T(8,128)(2,1)S(1)}, u32[]{:S(2)}, u32[]{:S(2)}) async-start(bf16[8,1,128,48]{2,3,1,0:T(8,128)(2,1)} %fusion.66), calls=%async_computation | async-start | bytes 196608 | tf_op jit(solution)/shard_map/all_to_all | solution.py:88
  20.2 9.8 %all-reduce = f32[4]{0:T(128)S(1)} all-reduce(f32[4]{0:T(128)S(1)} %dynamic-update-slice), channel_id=1, replica_groups=mesh['band'=4,'px'=4,'py'=2] {'band'}, use_global_device_ids=true, to_apply=%add | all-reduce | flops 4 | bytes 32
  30.0 8.4 %all-gather.2 = s32[4,2,256]{2,1,0:T(2,128)S(1)} all-gather(s32[1,2,256]{2,1,0:T(2,128)} %bitcast.281), channel_id=2, replica_groups=mesh['band'=4,'px'=4,'py'=2] {'px'}, dimensions={0}, use_global_device_ids=true | all-gather | bytes 10240 | tf_op jit(solution)/shard_map/all_gather | solution.py:92
  38.6 6.6 %all-gather.1 = bf16[32,1,128,48]{2,3,1,0:T(8,128)(2,1)S(1)} all-gather(bf16[8,1,128,48]{2,3,1,0:T(8,128)(2,1)S(1)} %all-to-all-done), channel_id=3, replica_groups=mesh['band'=4,'px'=4,'py'=2] {'px'}, dimensions={0}, use_global_device_ids=true | all-gather | bytes 491520 | tf_op jit(solution)/shard_map/all_gather | solution.py:89
  45.7 10.5 %fusion = f32[4,48,2,48,96,1]{4,1,5,3,2,0:T(8,128)} fusion(pred[4,256,48]{1,2,0:T(8,128)(4,1)S(1)} %iota_compare_fusion.1, bf16[4,256,2,96]{1,3,2,0:T(8,128)(2,1)S(1)} %broadcast_in_dim.37, s32[4,256]{1,0:T(4,128)S(1)} %bitcast.279, bf16[4,192,2,48,2]{1,3,2,4,0:T(8,128)(2,1)} %constant.95.clone, s32[]{:T(128)S(6)} %select_n.25), kind=kOutput, calls=%fused_computation | convolution fusion | flops 1897267200 | bytes 7622660 | tf_op jit(solution)/shard_map/psiwo,psixz->pwoxz/dot_general | solution.py:110
  56.3 11.2 %fusion.13 = bf16[4,48,2,48,96,1]{4,1,3,2,0,5:T(8,128)(2,1)} fusion(f32[4,48,2,48,96,1]{4,1,5,3,2,0:T(8,128)} %fusion, pred[4,256,48]{1,2,0:T(8,128)(4,1)S(1)} %iota_compare_fusion.1, bf16[4,256,2,96]{1,3,2,0:T(8,128)(2,1)S(1)} %broadcast_in_dim.37, s32[4,256]{1,0:T(4,128)S(1)} %bitcast.280, bf16[4,192,2,48,2]{1,3,2,4,0:T(8,128)(2,1)} %constant.94.clone, ...), kind=kOutput, calls=%fused_computation.16 | convolution fusion | flops 1900806144 | bytes 13520900 | tf_op jit(solution)/shard_map/psiwo,psixz->pwoxz/dot_general | solution.py:109
  67.5 6.2 %fusion.20 = f32[48,96,2,192,1,1]{3,1,5,4,2,0:T(8,128)S(1)} fusion(bf16[4,2,48,2,192,1]{4,2,0,1,3,5:T(8,128)(2,1)S(1)} %copy-done.10, bf16[4,48,2,48,96,1]{4,1,3,2,0,5:T(8,128)(2,1)} %fusion.13), kind=kOutput, calls=%fused_computation.25 | convolution fusion | flops 1358954496 | bytes 10911744 | tf_op jit(solution)/shard_map/pwoxz,poxtk->wztk/dot_general | solution.py:36
  88.4 14.6 %all_to_all.30 = f32[4,1,55296]{2,1,0:T(1,128)S(1)} all-to-all(f32[4,1,55296]{2,1,0:T(1,128)S(1)} %reshape.154), channel_id=1, replica_groups=mesh['band'=4,'px'=4,'py'=2] {'px'}, dimensions={0} | all-to-all | bytes 1769472 | tf_op jit(solution)/shard_map/all_to_all | solution.py:148
  116.1 4.4 %all-to-all-start.3 = ((bf16[4,2,27648]{2,1,0:T(2,128)(2,1)}), bf16[4,2,27648]{2,1,0:T(2,128)(2,1)S(1)}, u32[]{:S(2)}, u32[]{:S(2)}) async-start(bf16[4,2,27648]{2,1,0:T(2,128)(2,1)} %reshape.158), calls=%async_computation.3 | async-start | bytes 884736 | tf_op jit(solution)/shard_map/all_to_all | solution.py:154
  125.0 3.2 reshape.156
  128.3 3.9 %all-to-all-start.2 = ((f32[8,1,27648]{2,1,0:T(1,128)}), f32[8,1,27648]{2,1,0:T(1,128)S(1)}, u32[]{:S(2)}, u32[]{:S(2)}) async-start(f32[8,1,27648]{2,1,0:T(1,128)} %reshape.156), calls=%async_computation.2 | async-start | bytes 1769472 | tf_op jit(solution)/shard_map/all_to_all | solution.py:159
  137.0 41.7 %all-to-all-done.2 = f32[8,1,27648]{2,1,0:T(1,128)S(1)} async-done(((f32[8,1,27648]{2,1,0:T(1,128)}), f32[8,1,27648]{2,1,0:T(1,128)S(1)}, u32[]{:S(2)}, u32[]{:S(2)}) %all-to-all-start.2) | async-done | bytes 884768 | tf_op jit(solution)/shard_map/all_to_all | solution.py:159
  191.6 6.8 %reshape.160 = bf16[8,2,27648]{2,1,0:T(2,128)(2,1)} reshape(bf16[8,2,24,24,48]{4,3,2,1,0:T(8,128)(2,1)} %copy.81) | data formatting | bytes 1769472
  198.5 3.5 all-to-all-start.4
  202.8 29.8 %all-to-all-done.4 = bf16[8,2,27648]{2,1,0:T(2,128)(2,1)S(1)} async-done(((bf16[8,2,27648]{2,1,0:T(2,128)(2,1)}), bf16[8,2,27648]{2,1,0:T(2,128)(2,1)S(1)}, u32[]{:S(2)}, u32[]{:S(2)}) %all-to-all-start.4) | async-done | bytes 884768 | tf_op jit(solution)/shard_map/all_to_all | solution.py:182
  237.7 4.0 %reshape.104 = bf16[2,4,48,24,48]{2,1,4,3,0:T(4,128)(2,1)S(1)} reshape(bf16[2,192,24,48]{1,3,2,0:T(8,128)(2,1)} %fusion.50) | data formatting | bytes 1769472 | tf_op jit(solution)/shard_map/reshape | solution.py:185
  241.6 3.5 copy.84
  245.1 4.8 %reshape.162 = bf16[4,2,55296]{2,1,0:T(2,128)(2,1)S(1)} reshape(bf16[4,2,48,24,48]{4,3,2,1,0:T(8,128)(2,1)} %bitcast.271) | data formatting | bytes 1769472
  249.9 21.8 %all_to_all.31 = bf16[4,2,55296]{2,1,0:T(2,128)(2,1)S(1)} all-to-all(bf16[4,2,55296]{2,1,0:T(2,128)(2,1)S(1)} %reshape.162), channel_id=1, replica_groups=mesh['band'=4,'px'=4,'py'=2] {'px'}, dimensions={0} | all-to-all | bytes 1769472 | tf_op jit(solution)/shard_map/all_to_all | solution.py:186
  278.7 5.6 %fusion.62 = bf16[24,48,192]{2,1,0:T(8,128)(2,1)} fusion(f32[2,24,48,192]{3,2,1,0:T(8,128)} %copy-done.5, f32[48,24,192]{2,0,1:T(8,128)} %copy-done.6, f32[48,24,192]{2,0,1:T(8,128)} %copy-done.7, f32[48,24,192]{2,1,0:T(8,128)S(1)} %copy-done.4, f32[96,48,192]{2,1,0:T(8,128)} %param.27, s32[]{:T(128)S(6)} %select_n.27), kind=kLoop, calls=%fused_computation.70 | loop fusion | flops 5308416 | bytes 5750788 | tf_op jit(solution)/shard_map/convert_element_type | solution.py:118
  284.3 43.8 %all-gather.14.cloned.1.call-done = bf16[96,48,192]{2,1,0:T(8,128)(2,1)} async-done(((bf16[24,48,192]{2,1,0:T(8,128)(2,1)}), bf16[96,48,192]{2,1,0:T(8,128)(2,1)}) %all-gather.14.cloned.1.call-update) | async-done | bytes 1769488 | tf_op jit(solution)/shard_map/all_gather | solution.py:119
  328.1 10.5 %maximum_convert_fusion = f32[3,96,48,192]{3,2,1,0:T(8,128)} fusion(bf16[1,96,48,192]{3,2,1,0:T(8,128)(2,1)} %bitcast.276, bf16[1,96,48,192]{3,2,1,0:T(8,128)(2,1)} %bitcast.275, bf16[1,96,48,192]{3,2,1,0:T(8,128)(2,1)} %bitcast.274), kind=kLoop, calls=%fused_computation.15 | loop fusion | flops 7962624 | bytes 15925248 | tf_op jit(solution)/shard_map/stack | solution.py:191
  338.7 39.7 %all-gather.10.cloned.1.call-done = bf16[96,48,192]{2,1,0:T(8,128)(2,1)} async-done(((bf16[24,48,192]{2,1,0:T(8,128)(2,1)}), bf16[96,48,192]{2,1,0:T(8,128)(2,1)}) %all-gather.10.cloned.1.call-update) | async-done | bytes 1769488 | tf_op jit(solution)/shard_map/all_gather | solution.py:119
  378.3 4.5 %convert_element_type.89 = f32[96,48,192]{2,1,0:T(8,128)} convert(bf16[96,48,192]{2,1,0:T(8,128)(2,1)} %all-gather.10.cloned.1.call-done) | non-fusion elementwise | flops 884736 | bytes 5308416 | tf_op jit(solution)/shard_map/convert_element_type | solution.py:192
  (108 shorter events, 69.2 us)
Async XLA Ops:
  11.2 27.4 %all-to-all-start = ((bf16[8,1,128,48]{2,3,1,0:T(8,128)(2,1)}), bf16[8,1,128,48]{2,3,1,0:T(8,128)(2,1)S(1)}, u32[]{:S(2)}, u32[]{:S(2)}) async-start(bf16[8,1,128,48]{2,3,1,0:T(8,128)(2,1)} %fusion.66), calls=%async_computation | async-start | bytes 196608 | tf_op jit(solution)/shard_map/all_to_all | solution.py:88
  56.3 11.2 %copy-start.10 = (bf16[4,2,48,2,192,1]{4,2,0,1,3,5:T(8,128)(2,1)S(1)}, bf16[4,2,48,2,192,1]{4,2,0,1,3,5:T(8,128)(2,1)}, u32[]{:S(2)}) copy-start(bf16[4,2,48,2,192,1]{4,2,0,1,3,5:T(8,128)(2,1)} %constant.118) | copy-start | bytes 884740
  67.5 6.2 %copy-start.2 = (bf16[4,48,2,48,96,1]{4,1,3,2,0,5:T(8,128)(2,1)S(1)}, bf16[4,48,2,48,96,1]{4,1,3,2,0,5:T(8,128)(2,1)}, u32[]{:S(2)}) copy-start(bf16[4,48,2,48,96,1]{4,1,3,2,0,5:T(8,128)(2,1)} %fusion.13) | copy-start | bytes 10616836
  67.5 6.3 %copy-start.9 = (bf16[4,2,48,2,192,1]{4,2,0,1,3,5:T(8,128)(2,1)S(1)}, bf16[4,2,48,2,192,1]{4,2,0,1,3,5:T(8,128)(2,1)}, u32[]{:S(2)}) copy-start(bf16[4,2,48,2,192,1]{4,2,0,1,3,5:T(8,128)(2,1)} %constant.117) | copy-start | bytes 884740
  77.8 4.6 %copy-start.3 = (f32[48,24,192]{2,1,0:T(8,128)}, f32[48,24,192]{2,1,0:T(8,128)S(1)}, u32[]{:S(2)}) copy-start(f32[48,24,192]{2,1,0:T(8,128)S(1)} %fusion.18) | copy-start | bytes 2654212
  77.8 2.2 copy-start.8
  80.0 4.4 %copy-start.11 = (f32[192,4,48,1]{0,2,1,3:T(8,128)S(1)}, f32[192,4,48,1]{0,2,1,3:T(8,128)}, u32[]{:S(2)}) copy-start(f32[192,4,48,1]{0,2,1,3:T(8,128)} %constant.119) | copy-start | bytes 442372
  112.2 8.9 %copy-start.13 = (f32[192,192]{1,0:T(8,128)S(1)}, f32[192,192]{1,0:T(8,128)}, u32[]{:S(2)}) copy-start(f32[192,192]{1,0:T(8,128)} %constant.102.clone) | copy-start | bytes 442372
  116.1 12.2 %all-to-all-start.3 = ((bf16[4,2,27648]{2,1,0:T(2,128)(2,1)}), bf16[4,2,27648]{2,1,0:T(2,128)(2,1)S(1)}, u32[]{:S(2)}, u32[]{:S(2)}) async-start(bf16[4,2,27648]{2,1,0:T(2,128)(2,1)} %reshape.158), calls=%async_computation.3 | async-start | bytes 884736 | tf_op jit(solution)/shard_map/all_to_all | solution.py:154
  120.4 69.2 %all-gather.8.cloned.1.call-start = ((), (), s32[]{:S(2)}) async-start(), calls=%async_computation.6 | async-start | bytes 2949120 | tf_op jit(solution)/shard_map/all_gather | solution.py:119
  125.0 7.2 %copy-start.21 = (f32[192]{0:T(256)S(1)}, f32[192]{0:T(256)}, u32[]{:S(2)}) copy-start(f32[192]{0:T(256)} %constant.104.clone) | copy-start | bytes 2308
  128.3 5.9 %copy-start.15 = (bf16[192,4,48,1]{0,2,1,3:T(8,128)(2,1)S(1)}, bf16[192,4,48,1]{0,2,1,3:T(8,128)(2,1)}, u32[]{:S(2)}) copy-start(bf16[192,4,48,1]{0,2,1,3:T(8,128)(2,1)} %constant.123) | copy-start | bytes 221188
  128.3 50.4 %all-to-all-start.2 = ((f32[8,1,27648]{2,1,0:T(1,128)}), f32[8,1,27648]{2,1,0:T(1,128)S(1)}, u32[]{:S(2)}, u32[]{:S(2)}) async-start(f32[8,1,27648]{2,1,0:T(1,128)} %reshape.156), calls=%async_computation.2 | async-start | bytes 1769472 | tf_op jit(solution)/shard_map/all_to_all | solution.py:159
  132.2 2.5 copy-start.19
  137.0 45.4 %copy-start.12 = (f32[8,24,192,1]{2,1,0,3:T(8,128)S(1)}, f32[8,24,192,1]{2,1,0,3:T(8,128)}, u32[]{:S(2)}) copy-start(f32[8,24,192,1]{2,1,0,3:T(8,128)} %constant.116) | copy-start | bytes 442372
  137.0 45.4 %copy-start.20 = (f32[192,24]{0,1:T(8,128)S(1)}, f32[192,24]{0,1:T(8,128)}, u32[]{:S(2)}) copy-start(f32[192,24]{0,1:T(8,128)} %broadcast_add_fusion) | copy-start | bytes 55300
  198.5 34.2 %all-to-all-start.4 = ((bf16[8,2,27648]{2,1,0:T(2,128)(2,1)}), bf16[8,2,27648]{2,1,0:T(2,128)(2,1)S(1)}, u32[]{:S(2)}, u32[]{:S(2)}) async-start(bf16[8,2,27648]{2,1,0:T(2,128)(2,1)} %reshape.160), calls=%async_computation.4 | async-start | bytes 1769472 | tf_op jit(solution)/shard_map/all_to_all | solution.py:182
  202.0 32.9 %copy-start.18 = (bf16[192,8,24,1,1]{0,2,1,4,3:T(8,128)(2,1)S(1)}, bf16[192,8,24,1,1]{0,2,1,4,3:T(8,128)(2,1)}, u32[]{:S(2)}) copy-start(bf16[192,8,24,1,1]{0,2,1,4,3:T(8,128)(2,1)} %constant.125) | copy-start | bytes 221188
  202.0 82.3 %all-gather.12.cloned.1.call-start = ((), (), s32[]{:S(2)}) async-start(), calls=%async_computation.8 | async-start | bytes 2949120 | tf_op jit(solution)/shard_map/all_gather | solution.py:119
  202.8 125.4 %all-gather.14.cloned.1.call-start = ((), (), s32[]{:S(2)}) async-start(), calls=%async_computation.9 | async-start | bytes 2949120 | tf_op jit(solution)/shard_map/all_gather | solution.py:119
  249.9 24.2 %copy-start.16 = (bf16[192,4,48,1,1]{0,2,1,4,3:T(8,128)(2,1)S(1)}, bf16[192,4,48,1,1]{0,2,1,4,3:T(8,128)(2,1)}, u32[]{:S(2)}) copy-start(bf16[192,4,48,1,1]{0,2,1,4,3:T(8,128)(2,1)} %constant.127) | copy-start | bytes 221188
  277.2 1.5 copy-start.4
  278.1 100.2 %all-gather.10.cloned.1.call-start = ((), (), s32[]{:S(2)}) async-start(), calls=%async_computation.7 | async-start | bytes 2949120 | tf_op jit(solution)/shard_map/all_gather | solution.py:119
  328.1 54.7 %copy-start.1 = (bf16[1,128,384]{2,1,0:T(8,128)(2,1)S(1)}, bf16[1,128,384]{2,1,0:T(8,128)(2,1)}, u32[]{:S(2)}) copy-start(bf16[1,128,384]{2,1,0:T(8,128)(2,1)} %param.24) | copy-start | bytes 294916
  (7 other events, 7.4 us)
Sparse Core Ops, SparseCore 0:
  122.8 66.7 all-gather.7
  204.4 58.8 all-gather.11
  278.3 49.8 all-gather.13
  329.6 48.7 all-gather.9

commit v2 on v1

--- a/solution.py
+++ b/solution.py
@@ -1,9 +1,12 @@
+import functools
 import math
 
 import jax
 import jax.numpy as jnp
 import numpy as np
 from jax import lax
+from jax.experimental import pallas as pl
+from jax.experimental.pallas import tpu as pltpu
 from jax.experimental.layout import Layout, with_layout_constraint
 from jax.sharding import PartitionSpec as P
 
@@ -15,6 +18,8 @@
 BF = jnp.bfloat16
 F32 = jnp.float32
 HIGH = lax.Precision.HIGH
+CORE_LEAST = 0.05
+CORE_TYPICAL = 0.2
 
 
 def inverse_table(points):
@@ -90,7 +95,12 @@
     columns = columns.reshape(rows_px, groups, rows_py, bands_here, columns_here, 2, zshare)
     columns = columns.transpose(0, 2, 4, 5, 1, 3, 6).reshape(rows_px, sticks, 2, bands * zshare)
     places = lax.all_gather(stick_map, "px", axis=0, tiled=False)
-    weights = lax.all_gather(occupations, "band", axis=0, tiled=True)
+    loads = (orbitals.astype(F32) ** 2).sum((1, 2))
+    first = (px_index == 0) & (lax.axis_index("py") == 0)
+    own = jnp.where(jnp.arange(groups)[:, None] == lax.axis_index("band"), occupations[None, :], 0.0).reshape(bands)
+    totals = jnp.concatenate([jnp.where(first, own, 0.0), (occupations * loads).sum()[None]])
+    totals = lax.psum(totals, ("band", "px", "py"))
+    weights, mean = totals[:bands], totals[bands]
     y_hot = (places[:, 1, :, None] == jnp.arange(points, dtype=jnp.int32)).astype(BF)
     x_local = places[:, 0] - jnp.arange(rows_px, dtype=jnp.int32)[:, None] * xblock
     x_hot = x_local[:, :, None] == jnp.arange(xblock, dtype=jnp.int32)
@@ -111,12 +121,420 @@
     values = dot2("pwoxz,poxtk->wztk", plane.astype(BF), x_table)
     values = values.reshape(yblock, bands, zshare, 2, points)
     square = values[:, :, :, 0] * values[:, :, :, 0] + values[:, :, :, 1] * values[:, :, :, 1]
-    return (weights[None, :, None, None] * square).sum(1)
+    return (weights[None, :, None, None] * square).sum(1), mean
 
 
 def gathered(field):
     field = with_layout_constraint(field.astype(BF), Layout((0, 1, 2)))
     return lax.all_gather(field, "band", axis=0, tiled=True)
+
+
+LANES = 128
+HALF = 64
+
+
+def halves_stack(table, axis):
+    return jnp.asarray(np.concatenate([np.asarray(h) for h in two_halves(table)], axis))
+
+
+def packed_lane(parity, mode):
+    return np.where(mode < LANES, parity * LANES + mode, 2 * LANES + parity * HALF + mode - LANES)
+
+
+def chain_tables(points, rows_px, rows_py, groups):
+    basis, freq = real_basis(points)
+    derive = derivative_matrix(points)
+    xblock = points // rows_px
+    zshare = points // (rows_py * groups)
+    modes = np.arange(points)
+    forward = np.zeros((2, points, 3 * LANES + rows_px * LANES))
+    spread = np.zeros((rows_px, LANES, 3 * LANES))
+    for parity in range(2):
+        forward[parity][:, packed_lane(parity, modes)] = basis
+        lane = modes // xblock * LANES + parity * HALF + modes % xblock
+        forward[parity][:, 3 * LANES + lane] = basis
+        spread[modes // xblock, parity * HALF + modes % xblock, packed_lane(parity, modes)] = 1.0
+    source = np.arange(points // 2)
+    device, within = source // (zshare // 2), source % (zshare // 2)
+    even = device % rows_py * (points // rows_py) + device // rows_py * zshare + 2 * within
+    to_modes = [half for z in (even, even + 1) for half in two_halves(basis[z].T)]
+    from_modes = np.concatenate([basis[even], basis[even + 1]], 0)
+    return dict(
+        forward=jnp.stack([jnp.asarray(h) for h in two_halves(forward)]),
+        y_in=halves_stack(basis.T, 0),
+        y_out=halves_stack(basis, 0),
+        y_slope=halves_stack(derive.T, 0),
+        z_in=jnp.asarray(np.concatenate([np.asarray(h) for h in to_modes], 0)),
+        z_out=halves_stack(from_modes, 0),
+        spread=jnp.asarray(spread.astype(np.float32).astype(BF)),
+    )
+
+
+def slope_tables(points, rows_py, groups):
+    derive = derivative_matrix(points)
+    pairs = np.arange(points // 2)
+    zblock = points // rows_py
+    own = []
+    for py in range(rows_py):
+        order = np.concatenate([np.arange(zblock) + q * zblock for q in [py] + [q for q in range(rows_py) if q != py]])
+        mine = np.arange(zblock) + py * zblock
+        parts = []
+        for out_parity in range(2):
+            for in_parity in range(2):
+                parts.append(derive[np.ix_(order[in_parity::2], mine[out_parity::2])].T)
+        own.append(np.concatenate(parts, 0))
+    stacked = np.stack(own)
+    return np.concatenate([np.asarray(h) for h in two_halves(stacked)], 1)
+
+
+def final_tables(points):
+    basis, _ = real_basis(points)
+    derive = derivative_matrix(points)
+    out = np.zeros((2, 2 * LANES, 2, 2 * LANES))
+    for parity in range(2):
+        modes = np.arange(points)
+        row = np.where(modes < LANES, modes, parity * HALF + modes)
+        out[parity, row, 0, :points] = basis.T
+        out[parity, row, 1, :points] = basis.T @ derive
+    high, low = two_halves(out)
+    both = np.stack([np.asarray(high), np.asarray(low)], 3)
+    return jnp.asarray(both.reshape(2, 2 * LANES, 2, 4 * LANES).transpose(0, 2, 1, 3))
+
+
+def dotf(left, right):
+    return jnp.dot(left, right, preferred_element_type=F32)
+
+
+def split(value):
+    high = value.astype(BF)
+    return high, (value - high.astype(F32)).astype(BF)
+
+
+def chain_kernel(
+    dims, rho, forward, y_in, y_out, y_slope, z_in, z_out, spread, factor, slope,
+    xs, gy, gz, h,
+    others, c1s, c1, c2s, c2, c3s, c3, c4s, c4, gin, gs, wide, deep, sends, recvs,
+):
+    points, rows_px, rows_py, groups = dims
+    yblock = points // rows_px
+    zpairs = points // (rows_py * groups) // 2
+    pieces = groups * rows_py
+    kyblock = points // pieces
+    rows = zpairs * yblock
+    short = zpairs * kyblock
+    band, px, py = lax.axis_index("band"), lax.axis_index("px"), lax.axis_index("py")
+    me = band * rows_py + py
+    px_peers = [lax.rem(px + s, rows_px) for s in range(1, rows_px)]
+    zy_peers = [
+        (lax.rem(band + b, groups), lax.rem(py + q, rows_py))
+        for b in range(groups) for q in range(rows_py) if b or q
+    ]
+    barrier = pltpu.get_barrier_semaphore()
+    for peer in px_peers:
+        pl.semaphore_signal(barrier, inc=1, device_id=(band, peer, py), device_id_type=pl.DeviceIdType.MESH)
+    for peer_band, peer_py in zy_peers:
+        pl.semaphore_signal(barrier, inc=1, device_id=(peer_band, px, peer_py), device_id_type=pl.DeviceIdType.MESH)
+    pl.semaphore_wait(barrier, len(px_peers) + len(zy_peers))
+    used = []
+
+    def send(src, dst, device):
+        copy = pltpu.make_async_remote_copy(
+            src_ref=src, dst_ref=dst, send_sem=sends.at[len(used)], recv_sem=recvs.at[len(used)],
+            device_id=device, device_id_type=pl.DeviceIdType.MESH,
+        )
+        used.append(copy)
+        copy.start()
+        return copy
+
+    def to_px(src, dst):
+        return [send(src.at[peer], dst.at[px], (band, peer, py)) for peer in px_peers]
+
+    def to_zy(src, dst):
+        return [
+            send(src.at[b * rows_py + q], dst.at[me], (b, px, q)) for b, q in zy_peers
+        ]
+
+    def arrived(copies):
+        for copy in copies:
+            copy.wait_recv()
+
+    right, left = lax.rem(band + 1, groups), lax.rem(band + groups - 1, groups)
+
+    def to_band(field, slot, target):
+        return send(field.at[slot], field.at[slot], (target, px, py))
+
+    def to_other(slot):
+        return send(xs.at[slot], others.at[slot], (band, px, lax.rem(py + 1, rows_py)))
+
+    step = 2 * yblock
+
+    @pl.loop(0, rows // step)
+    def _(i):
+        at = pl.ds(pl.multiple_of(i * step, step), step)
+        out = None
+        for parity in range(2):
+            high, low = split(rho[parity, at, :])
+            part = dotf(high, forward[0, parity]) + dotf(low, forward[0, parity]) + dotf(high, forward[1, parity])
+            out = part if out is None else out + part
+        xs[band, at, :] = out[:, : 3 * LANES].astype(BF)
+        for p in range(rows_px):
+            c1s[p, at, :] = out[:, (3 + p) * LANES : (4 + p) * LANES].astype(BF)
+
+    first = to_px(c1s, c1)
+    ring_right = to_band(xs, band, right)
+    ring_left = to_band(xs, band, left)
+    across = [to_other(band)]
+    c1[px] = c1s[px]
+    arrived(first)
+
+    @pl.loop(0, zpairs // 2)
+    def _(i):
+        found = []
+        for k in range(2):
+            at = pl.ds(pl.multiple_of((2 * i + k) * yblock, yblock), yblock)
+            out = dotf(y_in[...], jnp.concatenate([c1[p, at, :] for p in range(rows_px)], 0))
+            found.append(out[:points] + out[points:])
+        at = pl.ds(pl.multiple_of(i * 2 * kyblock, 2 * kyblock), 2 * kyblock)
+        for d in range(pieces):
+            cut = slice(d * kyblock, (d + 1) * kyblock)
+            c2s[d, at, :] = jnp.concatenate([f[cut] for f in found], 0).astype(BF)
+
+    second = to_zy(c2s, c2)
+    c2[me] = c2s[me]
+    ring_right.wait_recv()
+    ring_far = to_band(xs, left, right)
+    across.append(to_other(left))
+    ring_left.wait_recv()
+    across.append(to_other(right))
+    arrived(second)
+    for d in range(pieces):
+        wide[pl.ds(d * short, short), :] = c2[d].astype(F32)
+    lane = lax.broadcasted_iota(jnp.int32, (points, LANES), 1)
+    column = pieces * zpairs
+
+    @pl.loop(0, kyblock)
+    def _(j):
+        data = wide[pl.ds(j, column, stride=kyblock), :].astype(BF)
+        out = dotf(z_in[...], data)
+        even = out[:points] + out[points : 2 * points]
+        odd = out[2 * points : 3 * points] + out[3 * points :]
+        spectrum = (even + pltpu.roll(odd, HALF, 1)) * factor[j]
+        spectrum = jnp.where(lane < HALF, spectrum, pltpu.roll(spectrum, HALF, 1))
+        high, low = split(spectrum)
+        back = dotf(z_out[...], high)
+        back = back[:points] + back[points:] + dotf(z_out[:points, :], low)
+        wide[pl.ds(j, column, stride=kyblock), :] = jnp.where(
+            lane[:column] < HALF, back[:column], back[column:]
+        )
+
+    for d in range(pieces):
+        c3s[d] = wide[pl.ds(d * short, short), :].astype(BF)
+    third = to_zy(c3s, c3)
+    c3[me] = c3s[me]
+    ring_far.wait_recv()
+    far = lax.rem(band + 2, groups)
+    across.append(to_other(far))
+    outward = to_px(xs, gin)
+    gin[px] = xs[px]
+    arrived(third)
+    for d in range(pieces):
+        wide[pl.ds(d * short, short), :] = c3[d].astype(F32)
+
+    @pl.loop(0, zpairs)
+    def _(i):
+        data = jnp.concatenate(
+            [wide[pl.ds(pl.multiple_of(d * short + i * kyblock, 8), kyblock), :] for d in range(pieces)], 0
+        ).astype(BF)
+        out = dotf(y_out[...], data)
+        out = out[:points] + out[points:]
+        at = pl.ds(pl.multiple_of(i * yblock, yblock), yblock)
+        for p in range(rows_px):
+            c4s[p, at, :] = out[p * yblock : (p + 1) * yblock].astype(BF)
+
+    fourth = to_px(c4s, c4)
+    c4[px] = c4s[px]
+    arrived(fourth)
+
+    @pl.loop(0, rows // step)
+    def _(i):
+        at = pl.ds(pl.multiple_of(i * step, step), step)
+        out = None
+        for p in range(rows_px):
+            part = dotf(c4[p, at, :], spread[p])
+            out = part if out is None else out + part
+        h[band, at, :] = out.astype(BF)
+
+    h_right = to_band(h, band, right)
+    h_left = to_band(h, band, left)
+    arrived(outward)
+
+    @pl.loop(0, zpairs)
+    def _(i):
+        at = pl.ds(pl.multiple_of(i * yblock, yblock), yblock)
+        out = dotf(y_slope[...], jnp.concatenate([gin[p, at, :] for p in range(rows_px)], 0))
+        out = out[:points] + out[points:]
+        for p in range(rows_px):
+            gs[p, at, :] = out[p * yblock : (p + 1) * yblock].astype(BF)
+
+    homeward = to_px(gs, gy)
+    gy[px] = gs[px]
+    h_right.wait_recv()
+    h_far = to_band(h, left, right)
+    arrived(across)
+    own_rows = groups * rows
+    for b in range(groups):
+        for t in range(3):
+            cut = pl.ds(t * LANES, LANES)
+            deep[t, pl.ds(b * rows, rows), :] = xs[b, :, cut].astype(F32)
+            deep[t, pl.ds(own_rows + b * rows, rows), :] = others[b, :, cut].astype(F32)
+    zlines = groups * zpairs
+    tail = lax.broadcasted_iota(jnp.int32, (zlines, LANES), 1) < HALF
+
+    @pl.loop(0, yblock)
+    def _(j):
+        data = [
+            deep[t, pl.ds(j, rows_py * zlines, stride=yblock), :].astype(BF) for t in range(3)
+        ]
+        out = [dotf(slope[...], d) for d in data]
+        parts = [
+            [out[t][q * zlines : (q + 1) * zlines] + out[t][(4 + q) * zlines : (5 + q) * zlines] for q in range(4)]
+            for t in range(3)
+        ]
+        even = parts[2][0] + pltpu.roll(parts[2][1], HALF, 1)
+        odd = pltpu.roll(parts[2][2], HALF, 1) + parts[2][3]
+        at = pl.ds(j, zlines, stride=yblock)
+        deep[0, at, :] = parts[0][0] + parts[1][1]
+        deep[1, at, :] = parts[0][2] + parts[1][3]
+        deep[2, at, :] = jnp.where(tail, even, odd)
+
+    for b in range(groups):
+        for t in range(3):
+            gz[b, :, pl.ds(t * LANES, LANES)] = deep[t, pl.ds(b * rows, rows), :].astype(BF)
+    h_left.wait_recv()
+    h_far.wait_recv()
+    arrived(homeward)
+    for copy in used:
+        copy.wait_send()
+
+
+def run_chain(rho, factor, slope, tables, dims):
+    points, rows_px, rows_py, groups = dims
+    yblock = points // rows_px
+    zpairs = points // (rows_py * groups) // 2
+    pieces = groups * rows_py
+    kyblock = points // pieces
+    rows, short = zpairs * yblock, zpairs * kyblock
+    copies = 4 * (rows_px - 1) + 2 * (pieces - 1) + 3 + 3 + groups
+    field = jax.ShapeDtypeStruct((groups, rows, 3 * LANES), BF)
+    vmem = pl.BlockSpec(memory_space=pltpu.VMEM)
+    lined = pltpu.VMEM((rows_px, rows, LANES), BF)
+    cut = pltpu.VMEM((pieces, short, LANES), BF)
+    names = ("forward", "y_in", "y_out", "y_slope", "z_in", "z_out", "spread")
+    return pl.pallas_call(
+        functools.partial(chain_kernel, dims),
+        out_shape=[field] * 4,
+        in_specs=[vmem] * (len(names) + 3),
+        out_specs=[vmem] * 4,
+        scratch_shapes=[
+            pltpu.VMEM((groups, rows, 3 * LANES), BF),
+            lined, lined, cut, cut, cut, cut, lined, lined,
+            pltpu.VMEM((rows_px, rows, 3 * LANES), BF),
+            pltpu.VMEM((rows_px, rows, 3 * LANES), BF),
+            pltpu.VMEM((pieces * short, LANES), F32),
+            pltpu.VMEM((3, rows_py * groups * rows, LANES), F32),
+            pltpu.SemaphoreType.DMA((copies,)),
+            pltpu.SemaphoreType.DMA((copies,)),
+        ],
+        compiler_params=pltpu.CompilerParams(
+            collective_id=1, has_side_effects=True, vmem_limit_bytes=60 << 20
+        ),
+    )(rho, *[tables[n] for n in names], factor, slope)
+
+
+def final_kernel(dims, shift, xs, gy, gz, h, table, potential, gradient):
+    points, yblock, pairs = dims
+    for parity in range(2):
+        first = slice(parity * LANES, (parity + 1) * LANES)
+
+        def natural(ref):
+            value = ref[...]
+            return jnp.concatenate([value[:, first], value[:, 2 * LANES :]], 1)
+
+        lines = natural(xs)
+        out = dotf(jnp.concatenate([lines, natural(gy), natural(gz), natural(h)], 0), table[parity, 0])
+        out = (out[:, : 2 * LANES] + out[:, 2 * LANES :])[:, :points]
+        grad_x = dotf(lines, table[parity, 1])
+        grad_x = (grad_x[:, : 2 * LANES] + grad_x[:, 2 * LANES :])[:, :points]
+        n = pairs * yblock
+        density, grad_y, grad_z, hartree = (out[k * n : (k + 1) * n] for k in range(4))
+        density = jnp.maximum(density + shift[0], CORE_LEAST)
+        cube_root = jnp.exp(jnp.log(density) * (1.0 / 3.0))
+        four_thirds = density * cube_root
+        grad_square = grad_x * grad_x + grad_y * grad_y + grad_z * grad_z
+        scale = (PBE_MU / (PBE_KAPPA * REDUCED_SCALE)) * grad_square
+        inverse = 1.0 / (four_thirds * four_thirds + scale)
+        ratio = four_thirds * four_thirds * inverse
+        steep = scale * inverse
+        part = (4.0 / 3.0) * (1.0 + PBE_KAPPA - PBE_KAPPA * ratio) - (8.0 / 3.0) * PBE_KAPPA * steep * ratio
+        value = hartree - SLATER_COEF * cube_root * part
+        for k in range(pairs):
+            cut = slice(k * yblock, (k + 1) * yblock)
+            potential[2 * k + parity] = value[cut]
+            gradient[0, 2 * k + parity] = grad_x[cut]
+            gradient[1, 2 * k + parity] = grad_y[cut]
+            gradient[2, 2 * k + parity] = grad_z[cut]
+
+
+def run_final(xs, gy, gz, h, shift, points, yblock):
+    groups, rows, _ = xs.shape
+    pairs = 2
+    steps = groups * rows // (pairs * yblock)
+    zblock = steps * 2 * pairs
+    table = final_tables(points)
+    flat = pl.BlockSpec((pairs * yblock, 3 * LANES), lambda i: (i, 0))
+    return pl.pallas_call(
+        functools.partial(final_kernel, (points, yblock, pairs)),
+        grid=(steps,),
+        out_shape=[
+            jax.ShapeDtypeStruct((zblock, yblock, points), F32),
+            jax.ShapeDtypeStruct((3, zblock, yblock, points), F32),
+        ],
+        in_specs=[pl.BlockSpec(memory_space=pltpu.SMEM)]
+        + [flat] * 4
+        + [pl.BlockSpec(table.shape, lambda i: (0, 0, 0, 0))],
+        out_specs=[
+            pl.BlockSpec((2 * pairs, yblock, points), lambda i: (i, 0, 0)),
+            pl.BlockSpec((3, 2 * pairs, yblock, points), lambda i: (0, i, 0, 0)),
+        ],
+    )(shift, *[f.reshape(groups * rows, 3 * LANES) for f in (xs, gy, gz, h)], table)
+
+
+def fast_body(orbitals, occupations, stick_map, core_density):
+    points = orbitals.shape[2] // 2
+    rows_px, rows_py, groups = lax.axis_size("px"), lax.axis_size("py"), lax.axis_size("band")
+    px_index, py_index, band_index = lax.axis_index("px"), lax.axis_index("py"), lax.axis_index("band")
+    dims = (points, rows_px, rows_py, groups)
+    yblock = xblock = points // rows_px
+    zshare = points // (rows_py * groups)
+    kyblock = points // (rows_py * groups)
+    density, mean = share_density(orbitals, occupations, stick_map, px_index)
+    core = lax.dynamic_slice_in_dim(core_density, band_index * zshare, zshare, 0)
+    shift = mean + CORE_TYPICAL
+    rho = density.transpose(1, 0, 2) + (core - shift)
+    rho = rho.reshape(zshare // 2, 2, yblock, points).transpose(1, 0, 2, 3).reshape(2, zshare // 2 * yblock, points)
+    _, freq = real_basis(points)
+    unit = 2.0 * math.pi / (points * SPACING)
+    all_q = (freq * freq).astype(np.float32)
+    lane_q = np.zeros((rows_px, LANES), np.float32)
+    lane_q[:, :xblock] = all_q.reshape(rows_px, xblock)
+    q_row = lax.dynamic_index_in_dim(jnp.asarray(lane_q), px_index, 0, keepdims=False)
+    q_col = lax.dynamic_slice_in_dim(jnp.asarray(all_q), (band_index * rows_py + py_index) * kyblock, kyblock)
+    squared = unit**2 * (q_col[:, None, None] + all_q[None, :, None] + q_row[None, None, :])
+    factor = jnp.where(squared > 0, 4.0 * math.pi / jnp.where(squared > 0, squared, 1.0), 0.0)
+    slope = lax.dynamic_index_in_dim(jnp.asarray(slope_tables(points, rows_py, groups)), py_index, 0, keepdims=False)
+    tables = chain_tables(points, rows_px, rows_py, groups)
+    xs, gy, gz, h = run_chain(rho, factor, slope, tables, dims)
+    return tuple(run_final(xs, gy, gz, h, shift.reshape(1), points, yblock))
 
 
 def body(orbitals, occupations, stick_map, core_density):
@@ -134,7 +552,7 @@
     pieces = groups * rows_py
     kyblock = points // pieces
 
-    density = share_density(orbitals, occupations, stick_map, px_index)
+    density, _ = share_density(orbitals, occupations, stick_map, px_index)
     core = lax.dynamic_slice_in_dim(core_density, band_index * zshare, zshare, 0)
     rho = density + core.transpose(1, 0, 2)
 
@@ -193,8 +611,18 @@
 
 
 def solution(mesh):
+    def step(orbitals, occupations, stick_map, core_density):
+        points = orbitals.shape[2] // 2
+        block = points // mesh.shape["px"]
+        share = points // (mesh.shape["py"] * mesh.shape["band"])
+        fits = (
+            points == LANES + HALF and block <= HALF and block % 16 == 0 and share % 8 == 0
+            and mesh.shape["py"] == 2 and mesh.shape["band"] == 4
+        )
+        return (fast_body if fits else body)(orbitals, occupations, stick_map, core_density)
+
     return jax.shard_map(
-        body,
+        step,
         mesh=mesh,
         in_specs=(P("band", ("px", "py"), None), P("band"), P(None, "px"), P("py", "px", None)),
         out_specs=(P("py", "px", None), P(None, "py", "px", None)),

time: 397 us -> 267 us (0.67)
  the two profiles are of different devices: /device:TPU:1 before, /device:TPU:17 now
where the time goes in v2:
time: 267 us; the launch traced here: 265 us
  Pallas kernels  155 us (58%)
  blocking collectives  53.8 us (20%)
  matrix products  33.5 us (13%)
  local copies, waits for them, and re-layouts  7.6 us (3%)
  other arithmetic  6.37 us (2%)
  starting transfers between devices  5.61 us (2%)
  between operations  2.75 us (1%)
    pallas_call x1, Pallas kernels, run_chain(): pl.pallas_call(functools.partial(chain_kernel, dims), out_shape=[field] *...  132 us
    psum x1, blocking collectives, share_density(): totals = lax.psum(totals, ('band', 'px', 'py'))  38.8 us
    pallas_call x1, Pallas kernels, run_final(): pl.pallas_call(functools.partial(final_kernel, (points, yblock, pairs)),...  23.3 us
    dot_general x1, matrix products, share_density(): jnp.einsum('psiwo,psixz->pwoxz', picked[0], spread, preferred_element_typ...  11.2 us
    dot_general x1, matrix products, share_density(): jnp.einsum('psiwo,psixz->pwoxz', picked[1], spread, preferred_element_typ...  10.7 us
    all_gather x1, blocking collectives, share_density(): columns = lax.all_gather(columns, 'px', axis=0, tiled=False)  8.57 us
    dot_general x2, matrix products, dot2(): return first + jnp.einsum(spec, data, low, preferred_element_type=F32)  7.59 us
    all_gather x1, blocking collectives, share_density(): places = lax.all_gather(stick_map, 'px', axis=0, tiled=False)  6.4 us
  transfers between devices with their start and end apart: 1, of which 0 were waited for; matrix products, arithmetic and copies ran while one was open for 4% of the time, Pallas kernels for 0%

profile of v2, /device:TPU:17, one launch (start us, length us, event | category | flops | bytes accessed | tf_op | source)
XLA Modules:
  0.0 264.7 jit_solution(2229839201785883680)
XLA Ops:
  0.6 1.2 fusion.48
  1.9 1.9 fusion.33
  3.8 5.6 %all-to-all-start = ((bf16[8,1,128,48]{2,3,1,0:T(8,128)(2,1)}), bf16[8,1,128,48]{2,3,1,0:T(8,128)(2,1)S(1)}, u32[]{:S(2)}, u32[]{:S(2)}) async-start(bf16[8,1,128,48]{2,3,1,0:T(8,128)(2,1)} %fusion.33), calls=%async_computation | async-start | bytes 196608 | tf_op jit(solution)/shard_map/all_to_all | solution.py:93
  9.4 1.6 multiply_reduce_fusion
  11.6 6.4 %all-gather.2 = s32[4,2,256]{2,1,0:T(2,128)S(1)} all-gather(s32[1,2,256]{2,1,0:T(2,128)} %bitcast.149), channel_id=2, replica_groups=mesh['band'=4,'px'=4,'py'=2] {'px'}, dimensions={0}, use_global_device_ids=true | all-gather | bytes 10240 | tf_op jit(solution)/shard_map/all_gather | solution.py:97
  18.1 0.8 dynamic_slice.24
  18.8 0.7 broadcast_add_fusion
  20.5 0.7 fusion.60
  21.2 1.9 compare_select_fusion.factor
  23.0 1.5 dynamic-slice_bitcast_fusion.slope
  24.5 38.8 %psum.7 = f32[5]{0:T(128)S(1)} all-reduce(f32[5]{0:T(128)S(1)} %pad_maximum_fusion), channel_id=1, replica_groups=mesh['band'=4,'px'=4,'py'=2] {'band','px','py'}, use_global_device_ids=true, to_apply=%region_1.2 | all-reduce | flops 5 | bytes 40 | tf_op jit(solution)/shard_map/psum | solution.py:102
  63.3 0.6 slice.20
  64.6 1.4 constant_dynamic-slice_fusion.1
  65.9 8.6 %all-gather.1 = bf16[32,1,128,48]{2,3,1,0:T(8,128)(2,1)S(1)} all-gather(bf16[8,1,128,48]{2,3,1,0:T(8,128)(2,1)S(1)} %all-to-all-done), channel_id=3, replica_groups=mesh['band'=4,'px'=4,'py'=2] {'px'}, dimensions={0}, use_global_device_ids=true | all-gather | bytes 491520 | tf_op jit(solution)/shard_map/all_gather | solution.py:94
  75.1 10.7 %fusion = f32[4,48,2,48,96,1]{4,1,5,3,2,0:T(8,128)} fusion(pred[4,256,48]{1,2,0:T(8,128)(4,1)S(1)} %iota_compare_fusion.1, bf16[4,256,2,96]{1,3,2,0:T(8,128)(2,1)S(1)} %broadcast_in_dim.58, s32[4,256]{1,0:T(4,128)S(1)} %bitcast.147, bf16[4,192,2,48,2]{1,3,2,4,0:T(8,128)(2,1)} %constant.93.clone, s32[]{:T(128)S(6)} %select_n.46), kind=kOutput, calls=%fused_computation | convolution fusion | flops 1897267200 | bytes 7622660 | tf_op jit(solution)/shard_map/psiwo,psixz->pwoxz/dot_general | solution.py:120
  85.8 11.2 %fusion.13 = bf16[4,48,2,48,96,1]{4,1,3,2,0,5:T(8,128)(2,1)} fusion(f32[4,48,2,48,96,1]{4,1,5,3,2,0:T(8,128)} %fusion, pred[4,256,48]{1,2,0:T(8,128)(4,1)S(1)} %iota_compare_fusion.1, bf16[4,256,2,96]{1,3,2,0:T(8,128)(2,1)S(1)} %broadcast_in_dim.58, s32[4,256]{1,0:T(4,128)S(1)} %bitcast.148, bf16[4,192,2,48,2]{1,3,2,4,0:T(8,128)(2,1)} %constant.92.clone, ...), kind=kOutput, calls=%fused_computation.15 | convolution fusion | flops 1900806144 | bytes 13520900 | tf_op jit(solution)/shard_map/psiwo,psixz->pwoxz/dot_general | solution.py:119
  97.1 5.7 %fusion.20 = f32[48,96,2,192,1,1]{3,1,5,4,2,0:T(8,128)S(1)} fusion(bf16[4,2,48,2,192,1]{4,2,0,1,3,5:T(8,128)(2,1)S(1)} %copy-done.2, bf16[4,48,2,48,96,1]{4,1,3,2,0,5:T(8,128)(2,1)} %fusion.13), kind=kOutput, calls=%fused_computation.24 | convolution fusion | flops 1358954496 | bytes 10911744 | tf_op jit(solution)/shard_map/pwoxz,poxtk->wztk/dot_general | solution.py:41
  102.8 2.7 %bitcast_add_fusion = f32[48,96,2,192]{3,1,2,0:T(8,128)S(1)} fusion(f32[48,96,2,192,1,1]{3,1,5,4,2,0:T(8,128)S(1)} %fusion.20, bf16[4,2,48,2,192,1]{4,2,0,1,3,5:T(8,128)(2,1)S(1)} %copy-done.1, bf16[4,48,2,48,96,1]{4,1,3,2,0,5:T(8,128)(2,1)S(1)} %copy-done), kind=kOutput, calls=%fused_computation.8 | convolution fusion | flops 1360723968 | bytes 17989632 | tf_op jit(solution)/shard_map/pwoxz,poxtk->wztk/dot_general | solution.py:40
  105.6 1.2 fusion.18
  106.8 0.7 fusion.31
  107.5 0.7 reshape.123
  108.2 1.4 copy.39
  109.6 131.8 %shard_map.230 = (bf16[4,576,384]{2,1,0:T(8,128)(2,1)}, bf16[4,576,384]{2,1,0:T(8,128)(2,1)}, bf16[4,576,384]{2,1,0:T(8,128)(2,1)}, bf16[4,576,384]{2,1,0:T(8,128)(2,1)}) custom-call(f32[2,576,192]{2,1,0:T(8,128)} %bitcast.140, bf16[2,2,192,896]{3,2,1,0:T(8,128)(2,1)} %constant.113.forward, bf16[384,192]{1,0:T(8,128)(2,1)} %constant.102.clone.y_in, ...), custom_call_target="tpu_custom_call" | custom-call | tf_op jit(solution)/shard_map/pallas_call | solution.py:433
  241.4 23.3 %shard_map.231 = (f32[96,48,192]{2,1,0:T(8,128)}, f32[3,96,48,192]{3,2,1,0:T(8,128)}) custom-call(f32[1]{0:T(128)} %add.83.shift, bf16[2304,384]{1,0:T(8,128)(2,1)} %bitcast.141, bf16[2304,384]{1,0:T(8,128)(2,1)} %bitcast.142, bf16[2304,384]{1,0:T(8,128)(2,1)} %bitcast.143, bf16[2304,384]{1,0:T(8,128)(2,1)} %bitcast.144, ...), custom_call_target="tpu_custom_call" | custom-call | tf_op jit(solution)/shard_map/pallas_call | solution.py:495
  (16 shorter events, 0.8 us)
Async XLA Ops:
  3.8 62.2 %all-to-all-start = ((bf16[8,1,128,48]{2,3,1,0:T(8,128)(2,1)}), bf16[8,1,128,48]{2,3,1,0:T(8,128)(2,1)S(1)}, u32[]{:S(2)}, u32[]{:S(2)}) async-start(bf16[8,1,128,48]{2,3,1,0:T(8,128)(2,1)} %fusion.33), calls=%async_computation | async-start | bytes 196608 | tf_op jit(solution)/shard_map/all_to_all | solution.py:93
  85.8 11.2 %copy-start.2 = (bf16[4,2,48,2,192,1]{4,2,0,1,3,5:T(8,128)(2,1)S(1)}, bf16[4,2,48,2,192,1]{4,2,0,1,3,5:T(8,128)(2,1)}, u32[]{:S(2)}) copy-start(bf16[4,2,48,2,192,1]{4,2,0,1,3,5:T(8,128)(2,1)} %constant.116) | copy-start | bytes 884740
  97.1 5.7 %copy-start = (bf16[4,48,2,48,96,1]{4,1,3,2,0,5:T(8,128)(2,1)S(1)}, bf16[4,48,2,48,96,1]{4,1,3,2,0,5:T(8,128)(2,1)}, u32[]{:S(2)}) copy-start(bf16[4,48,2,48,96,1]{4,1,3,2,0,5:T(8,128)(2,1)} %fusion.13) | copy-start | bytes 10616836
  97.1 5.7 %copy-start.1 = (bf16[4,2,48,2,192,1]{4,2,0,1,3,5:T(8,128)(2,1)S(1)}, bf16[4,2,48,2,192,1]{4,2,0,1,3,5:T(8,128)(2,1)}, u32[]{:S(2)}) copy-start(bf16[4,2,48,2,192,1]{4,2,0,1,3,5:T(8,128)(2,1)} %constant.115) | copy-start | bytes 884740

commit v3 on v2

--- a/solution.py
+++ b/solution.py
@@ -157,14 +157,14 @@
     source = np.arange(points // 2)
     device, within = source // (zshare // 2), source % (zshare // 2)
     even = device % rows_py * (points // rows_py) + device // rows_py * zshare + 2 * within
-    to_modes = [half for z in (even, even + 1) for half in two_halves(basis[z].T)]
+    to_modes = np.concatenate([basis[even].T, basis[even + 1].T], 0)
     from_modes = np.concatenate([basis[even], basis[even + 1]], 0)
     return dict(
         forward=jnp.stack([jnp.asarray(h) for h in two_halves(forward)]),
         y_in=halves_stack(basis.T, 0),
         y_out=halves_stack(basis, 0),
         y_slope=halves_stack(derive.T, 0),
-        z_in=jnp.asarray(np.concatenate([np.asarray(h) for h in to_modes], 0)),
+        z_in=halves_stack(to_modes, 1),
         z_out=halves_stack(from_modes, 0),
         spread=jnp.asarray(spread.astype(np.float32).astype(BF)),
     )
@@ -184,7 +184,7 @@
                 parts.append(derive[np.ix_(order[in_parity::2], mine[out_parity::2])].T)
         own.append(np.concatenate(parts, 0))
     stacked = np.stack(own)
-    return np.concatenate([np.asarray(h) for h in two_halves(stacked)], 1)
+    return np.concatenate([np.asarray(h) for h in two_halves(stacked)], 2)
 
 
 def final_tables(points):
@@ -197,8 +197,8 @@
         out[parity, row, 0, :points] = basis.T
         out[parity, row, 1, :points] = basis.T @ derive
     high, low = two_halves(out)
-    both = np.stack([np.asarray(high), np.asarray(low)], 3)
-    return jnp.asarray(both.reshape(2, 2 * LANES, 2, 4 * LANES).transpose(0, 2, 1, 3))
+    both = np.stack([np.asarray(high), np.asarray(low)], 0)
+    return jnp.asarray(both.transpose(1, 3, 0, 2, 4))
 
 
 def dotf(left, right):
@@ -211,7 +211,7 @@
 
 
 def chain_kernel(
-    dims, rho, forward, y_in, y_out, y_slope, z_in, z_out, spread, factor, slope,
+    dims, rho, forward, y_in, y_out, y_slope, z_in, z_out, spread, slope,
     xs, gy, gz, h,
     others, c1s, c1, c2s, c2, c3s, c3, c4s, c4, gin, gs, wide, deep, sends, recvs,
 ):
@@ -282,7 +282,6 @@
 
     first = to_px(c1s, c1)
     ring_right = to_band(xs, band, right)
-    ring_left = to_band(xs, band, left)
     across = [to_other(band)]
     c1[px] = c1s[px]
     arrived(first)
@@ -301,36 +300,51 @@
 
     second = to_zy(c2s, c2)
     c2[me] = c2s[me]
+    ring_left = to_band(xs, band, left)
     ring_right.wait_recv()
     ring_far = to_band(xs, left, right)
     across.append(to_other(left))
-    ring_left.wait_recv()
-    across.append(to_other(right))
     arrived(second)
     for d in range(pieces):
         wide[pl.ds(d * short, short), :] = c2[d].astype(F32)
-    lane = lax.broadcasted_iota(jnp.int32, (points, LANES), 1)
+    lane = lax.broadcasted_iota(jnp.int32, (points, 2 * LANES), 1) % LANES
     column = pieces * zpairs
-
-    @pl.loop(0, kyblock)
-    def _(j):
-        data = wide[pl.ds(j, column, stride=kyblock), :].astype(BF)
-        out = dotf(z_in[...], data)
-        even = out[:points] + out[points : 2 * points]
-        odd = out[2 * points : 3 * points] + out[3 * points :]
-        spectrum = (even + pltpu.roll(odd, HALF, 1)) * factor[j]
-        spectrum = jnp.where(lane < HALF, spectrum, pltpu.roll(spectrum, HALF, 1))
+    unit = 2.0 * math.pi / (points * SPACING)
+
+    def frequency(index):
+        return jnp.where(index > points // 2, index - points // 2, index)
+
+    level = frequency(lax.broadcasted_iota(jnp.int32, (points, 2 * LANES), 0))
+    across_x = frequency(lane + px * yblock)
+    flat = (level * level + across_x * across_x).astype(F32)
+    second_half = lax.broadcasted_iota(jnp.int32, (points, 2 * LANES), 1) >= LANES
+
+    def swapped(value):
+        return jnp.concatenate([pltpu.roll(value[:, k * LANES : (k + 1) * LANES], HALF, 1) for k in range(2)], 1)
+
+    @pl.loop(0, kyblock // 2)
+    def _(i):
+        at = [pl.ds(2 * i + k, column, stride=kyblock) for k in range(2)]
+        data = jnp.concatenate([wide[a, :] for a in at], 1).astype(BF)
+        out = dotf(z_in[...], jnp.concatenate([data, data], 0))
+        here = [frequency(me * kyblock + 2 * i + k) for k in range(2)]
+        here = [(f * f).astype(F32) for f in here]
+        squared = unit**2 * (flat + jnp.where(second_half, here[1], here[0]))
+        factor = jnp.where(squared > 0, 4.0 * math.pi / jnp.where(squared > 0, squared, 1.0), 0.0)
+        spectrum = (out[:points] + swapped(out[points:])) * factor
+        spectrum = jnp.where(lane < HALF, spectrum, swapped(spectrum))
         high, low = split(spectrum)
-        back = dotf(z_out[...], high)
-        back = back[:points] + back[points:] + dotf(z_out[:points, :], low)
-        wide[pl.ds(j, column, stride=kyblock), :] = jnp.where(
-            lane[:column] < HALF, back[:column], back[column:]
-        )
+        back = dotf(z_out[:points, :], high) + dotf(z_out[points:, :], high) + dotf(z_out[:points, :], low)
+        back = jnp.where(lane[:column] < HALF, back[:column], back[column:])
+        for k in range(2):
+            wide[at[k], :] = back[:, k * LANES : (k + 1) * LANES]
 
     for d in range(pieces):
         c3s[d] = wide[pl.ds(d * short, short), :].astype(BF)
     third = to_zy(c3s, c3)
     c3[me] = c3s[me]
+    ring_left.wait_recv()
+    across.append(to_other(right))
     ring_far.wait_recv()
     far = lax.rem(band + 2, groups)
     across.append(to_other(far))
@@ -390,22 +404,25 @@
     zlines = groups * zpairs
     tail = lax.broadcasted_iota(jnp.int32, (zlines, LANES), 1) < HALF
 
-    @pl.loop(0, yblock)
-    def _(j):
-        data = [
-            deep[t, pl.ds(j, rows_py * zlines, stride=yblock), :].astype(BF) for t in range(3)
-        ]
-        out = [dotf(slope[...], d) for d in data]
-        parts = [
-            [out[t][q * zlines : (q + 1) * zlines] + out[t][(4 + q) * zlines : (5 + q) * zlines] for q in range(4)]
-            for t in range(3)
-        ]
-        even = parts[2][0] + pltpu.roll(parts[2][1], HALF, 1)
-        odd = pltpu.roll(parts[2][2], HALF, 1) + parts[2][3]
-        at = pl.ds(j, zlines, stride=yblock)
-        deep[0, at, :] = parts[0][0] + parts[1][1]
-        deep[1, at, :] = parts[0][2] + parts[1][3]
-        deep[2, at, :] = jnp.where(tail, even, odd)
+    @pl.loop(0, yblock // 2)
+    def _(i):
+        data = jnp.concatenate(
+            [
+                deep[t, pl.ds(2 * i + k, rows_py * zlines, stride=yblock), :]
+                for k in range(2) for t in range(3)
+            ],
+            1,
+        ).astype(BF)
+        out = dotf(slope[py], jnp.concatenate([data, data], 0))
+        parts = [out[q * zlines : (q + 1) * zlines] for q in range(4)]
+        for k in range(2):
+            first, middle, last = (slice((3 * k + t) * LANES, (3 * k + t + 1) * LANES) for t in range(3))
+            at = pl.ds(2 * i + k, zlines, stride=yblock)
+            even = parts[0][:, last] + pltpu.roll(parts[1][:, last], HALF, 1)
+            odd = pltpu.roll(parts[2][:, last], HALF, 1) + parts[3][:, last]
+            deep[0, at, :] = parts[0][:, first] + parts[1][:, middle]
+            deep[1, at, :] = parts[2][:, first] + parts[3][:, middle]
+            deep[2, at, :] = jnp.where(tail, even, odd)
 
     for b in range(groups):
         for t in range(3):
@@ -417,7 +434,7 @@
         copy.wait_send()
 
 
-def run_chain(rho, factor, slope, tables, dims):
+def run_chain(rho, slope, tables, dims):
     points, rows_px, rows_py, groups = dims
     yblock = points // rows_px
     zpairs = points // (rows_py * groups) // 2
@@ -433,7 +450,7 @@
     return pl.pallas_call(
         functools.partial(chain_kernel, dims),
         out_shape=[field] * 4,
-        in_specs=[vmem] * (len(names) + 3),
+        in_specs=[vmem] * (len(names) + 2),
         out_specs=[vmem] * 4,
         scratch_shapes=[
             pltpu.VMEM((groups, rows, 3 * LANES), BF),
@@ -448,7 +465,7 @@
         compiler_params=pltpu.CompilerParams(
             collective_id=1, has_side_effects=True, vmem_limit_bytes=60 << 20
         ),
-    )(rho, *[tables[n] for n in names], factor, slope)
+    )(rho, *[tables[n] for n in names], slope)
 
 
 def final_kernel(dims, shift, xs, gy, gz, h, table, potential, gradient):
@@ -460,14 +477,16 @@
             value = ref[...]
             return jnp.concatenate([value[:, first], value[:, 2 * LANES :]], 1)
 
+        def spatial(value, kind):
+            out = dotf(value, table[parity, kind, 0]) + dotf(value, table[parity, kind, 1])
+            return out[:, :points]
+
         lines = natural(xs)
-        out = dotf(jnp.concatenate([lines, natural(gy), natural(gz), natural(h)], 0), table[parity, 0])
-        out = (out[:, : 2 * LANES] + out[:, 2 * LANES :])[:, :points]
-        grad_x = dotf(lines, table[parity, 1])
-        grad_x = (grad_x[:, : 2 * LANES] + grad_x[:, 2 * LANES :])[:, :points]
+        out = spatial(jnp.concatenate([lines, natural(gy), natural(gz), natural(h)], 0), 0)
+        grad_x = spatial(lines, 1)
         n = pairs * yblock
         density, grad_y, grad_z, hartree = (out[k * n : (k + 1) * n] for k in range(4))
-        density = jnp.maximum(density + shift[0], CORE_LEAST)
+        density = jnp.maximum(density + shift[0:1, 0:1], CORE_LEAST)
         cube_root = jnp.exp(jnp.log(density) * (1.0 / 3.0))
         four_thirds = density * cube_root
         grad_square = grad_x * grad_x + grad_y * grad_y + grad_z * grad_z
@@ -499,9 +518,9 @@
             jax.ShapeDtypeStruct((zblock, yblock, points), F32),
             jax.ShapeDtypeStruct((3, zblock, yblock, points), F32),
         ],
-        in_specs=[pl.BlockSpec(memory_space=pltpu.SMEM)]
+        in_specs=[pl.BlockSpec((8, LANES), lambda i: (0, 0))]
         + [flat] * 4
-        + [pl.BlockSpec(table.shape, lambda i: (0, 0, 0, 0))],
+        + [pl.BlockSpec(table.shape, lambda i: (0, 0, 0, 0, 0))],
         out_specs=[
             pl.BlockSpec((2 * pairs, yblock, points), lambda i: (i, 0, 0)),
             pl.BlockSpec((3, 2 * pairs, yblock, points), lambda i: (0, i, 0, 0)),
@@ -509,32 +528,217 @@
     )(shift, *[f.reshape(groups * rows, 3 * LANES) for f in (xs, gy, gz, h)], table)
 
 
+def column_tables(points, rows_px, rows_py, groups):
+    inverse = inverse_table(points)
+    pieces = groups * rows_py
+    zshare = points // pieces
+    yblock = points // rows_px
+    doubled = 2 * points
+    z_order = inverse.reshape(2, points, 2, rows_py, groups, zshare).transpose(0, 1, 4, 3, 2, 5)
+    by_y = np.zeros((rows_px, 2, points, 2, HALF))
+    by_y[:, :, :, :, :yblock] = inverse.reshape(2, points, 2, rows_px, yblock).transpose(3, 0, 1, 2, 4)
+    by_y = np.concatenate([np.asarray(h) for h in two_halves(by_y.reshape(rows_px, 2, points, LANES))], 3)
+    by_x = np.stack([np.asarray(h) for h in two_halves(inverse[0].transpose(1, 2, 0))], 1)
+    z_table = np.stack([np.asarray(h) for h in two_halves(z_order.reshape(doubled, doubled).T)])
+    return jnp.asarray(z_table), jnp.asarray(by_y), jnp.asarray(by_x)
+
+
+def column_kernel(
+    dims, occupation, orbitals, z_table, places, sticks, every_place, notes, columns, note, middle, sends, recvs
+):
+    points, rows_px, rows_py, groups = dims
+    band, px, py = lax.axis_index("band"), lax.axis_index("px"), lax.axis_index("py")
+    me = band * rows_py + py
+    px_peers = [(band, lax.rem(px + s, rows_px), py) for s in range(1, rows_px)]
+    zy_peers = [
+        (lax.rem(band + b, groups), px, lax.rem(py + q, rows_py))
+        for b in range(groups) for q in range(rows_py) if b or q
+    ]
+    barrier = pltpu.get_barrier_semaphore()
+    for peer in px_peers + zy_peers:
+        pl.semaphore_signal(barrier, inc=1, device_id=peer, device_id_type=pl.DeviceIdType.MESH)
+    coefficients = orbitals[0]
+    contract = (((1,), (1,)), ((), ()))
+    found = lax.dot_general(z_table[0], coefficients, contract, preferred_element_type=F32)
+    found = found + lax.dot_general(z_table[1], coefficients, contract, preferred_element_type=F32)
+    share = 2 * points // (groups * rows_py)
+    for d in range(groups * rows_py):
+        columns[d] = found[d * share : (d + 1) * share].astype(BF)
+    wide = coefficients.astype(F32)
+    load = occupation[0] * jnp.sum(wide * wide)
+    lane = lax.broadcasted_iota(jnp.int32, (8, LANES), 1)
+    note[...] = jnp.where(lane == 0, occupation[0], jnp.where(lane == 1, load, 0.0))
+    pl.semaphore_wait(barrier, len(px_peers) + len(zy_peers))
+    used = []
+
+    def send(src, dst, device):
+        copy = pltpu.make_async_remote_copy(
+            src_ref=src, dst_ref=dst, send_sem=sends.at[len(used)], recv_sem=recvs.at[len(used)],
+            device_id=device, device_id_type=pl.DeviceIdType.MESH,
+        )
+        used.append(copy)
+        copy.start()
+
+    for peer in zy_peers:
+        send(columns.at[peer[0] * rows_py + peer[2]], middle.at[me], peer)
+    for peer in zy_peers:
+        send(note, notes.at[px, me], peer)
+    first = len(used)
+    for peer in px_peers:
+        send(places, every_place.at[px], peer)
+    middle[me] = columns[me]
+    notes[px, me] = note[...]
+    every_place[px] = places[...]
+    for copy in used[:first]:
+        copy.wait_recv()
+    for peer in px_peers:
+        send(middle, sticks.at[px], peer)
+        send(notes.at[px], notes.at[px], peer)
+    sticks[px] = middle[...]
+    for copy in used[first:]:
+        copy.wait_recv()
+    for copy in used:
+        copy.wait_send()
+
+
+def run_columns(occupations, orbitals, z_table, places, dims):
+    points, rows_px, rows_py, groups = dims
+    pieces = groups * rows_py
+    copies = 2 * (pieces - 1) + 3 * (rows_px - 1)
+    share = (pieces, 2 * points // pieces, LANES)
+    vmem = pl.BlockSpec(memory_space=pltpu.VMEM)
+    return pl.pallas_call(
+        functools.partial(column_kernel, dims),
+        out_shape=[
+            jax.ShapeDtypeStruct((rows_px,) + share, BF),
+            jax.ShapeDtypeStruct((rows_px,) + places.shape, jnp.int32),
+            jax.ShapeDtypeStruct((rows_px, pieces, 8, LANES), F32),
+        ],
+        in_specs=[pl.BlockSpec(memory_space=pltpu.SMEM)] + [vmem] * 3,
+        out_specs=[vmem] * 3,
+        scratch_shapes=[
+            pltpu.VMEM(share, BF),
+            pltpu.VMEM((8, LANES), F32),
+            pltpu.VMEM(share, BF),
+            pltpu.SemaphoreType.DMA((copies,)),
+            pltpu.SemaphoreType.DMA((copies,)),
+        ],
+        compiler_params=pltpu.CompilerParams(collective_id=2, has_side_effects=True),
+    )(occupations, orbitals, z_table, places)
+
+
+def density_kernel(dims, notes, sticks, places, by_y, by_x, core, rho, shift, wide, planes, held, sem):
+    points, rows_px, rows_py, groups = dims
+    xblock = yblock = points // rows_px
+    zshare = points // (rows_py * groups)
+    band, px = lax.axis_index("band"), lax.axis_index("px")
+    fetch = pltpu.make_async_copy(core.at[pl.ds(band * zshare, zshare)], held, sem)
+    fetch.start()
+    mean = CORE_TYPICAL
+    for p in range(rows_px):
+        for d in range(groups * rows_py):
+            mean = mean + notes[p, d, :, 1:2]
+    shift[...] = jnp.broadcast_to(mean, (8, LANES))
+    mean = mean[0:1]
+    weights = [notes[0, b * rows_py, 0:1, 0:1] for b in range(groups)]
+    count = 8
+    lines = groups * zshare
+    sticks_px = rows_py * LANES
+
+    @pl.loop(0, rows_px)
+    def _(p):
+        wide[...] = sticks[p].astype(F32)
+        spots = places[p]
+        at_y = lax.broadcasted_iota(jnp.int32, (points, sticks_px), 0) == spots[1:2, :]
+        one_hot = at_y.astype(F32).astype(BF)
+        table = jnp.concatenate(
+            [
+                lax.dot_general(one_hot, by_y[px, i], (((0,), (0,)), ((), ())), preferred_element_type=F32)
+                for i in range(2)
+            ],
+            0,
+        ).astype(BF)
+        at_x = lax.broadcasted_iota(jnp.int32, (xblock, sticks_px), 0) == spots[0:1, :] - p * xblock
+        mask = at_x.astype(F32)
+
+        @pl.loop(0, lines // count)
+        def _(c):
+            b = c // (zshare // count)
+            z = (c % (zshare // count)) * count
+            blocks = []
+            for k in range(count):
+                tiles = [
+                    mask[:, q * LANES : (q + 1) * LANES]
+                    * wide[b * rows_py + q, pl.ds(i * zshare + z + k, 1), :]
+                    for i in range(2) for q in range(rows_py)
+                ]
+                blocks.append(jnp.concatenate(tiles, 1))
+            out = dotf(jnp.concatenate(blocks, 0).astype(BF), table)
+            out = (out[:, :LANES] + out[:, LANES:]).astype(BF)
+            for k in range(count):
+                planes[c * count + k, pl.ds(pl.multiple_of(p * xblock, xblock), xblock), :] = out[
+                    k * xblock : (k + 1) * xblock
+                ]
+
+    fetch.wait()
+    lane = lax.broadcasted_iota(jnp.int32, (points, LANES), 1)
+    sign = jnp.where(lane < HALF, -1.0, 1.0)
+
+    @pl.loop(0, zshare // 2)
+    def _(i):
+        total = [None, None]
+        for b in range(groups):
+            both = jnp.concatenate([planes[b * zshare + 2 * i + k] for k in range(2)], 1)
+            cosine = dotf(by_x[0, 0], both) + dotf(by_x[0, 1], both)
+            sine = dotf(by_x[1, 0], both) + dotf(by_x[1, 1], both)
+            for k in range(2):
+                cut = slice(k * LANES, (k + 1) * LANES)
+                value = cosine[:, cut] + sign * pltpu.roll(sine[:, cut], HALF, 1)
+                value = weights[b] * (value * value)
+                total[k] = value if b == 0 else total[k] + value
+        for k in range(2):
+            density = total[k] + pltpu.roll(total[k], HALF, 1)
+            rho[k, pl.ds(pl.multiple_of(i * yblock, yblock), yblock), :] = (
+                density.T[:yblock] + (held[2 * i + k] - mean)
+            )
+
+
+def run_density(notes, sticks, places, core, by_y, by_x, dims):
+    points, rows_px, rows_py, groups = dims
+    zshare = points // (rows_py * groups)
+    yblock = points // rows_px
+    vmem = pl.BlockSpec(memory_space=pltpu.VMEM)
+    return pl.pallas_call(
+        functools.partial(density_kernel, dims),
+        out_shape=[
+            jax.ShapeDtypeStruct((2, zshare // 2 * yblock, points), F32),
+            jax.ShapeDtypeStruct((8, LANES), F32),
+        ],
+        in_specs=[vmem] * 5 + [pl.BlockSpec(memory_space=pl.ANY)],
+        out_specs=[vmem] * 2,
+        scratch_shapes=[
+            pltpu.VMEM(sticks.shape[1:], F32),
+            pltpu.VMEM((groups * zshare, points, LANES), BF),
+            pltpu.VMEM((zshare, yblock, points), F32),
+            pltpu.SemaphoreType.DMA,
+        ],
+        compiler_params=pltpu.CompilerParams(vmem_limit_bytes=48 << 20),
+    )(notes, sticks, places, by_y, by_x, core)
+
+
 def fast_body(orbitals, occupations, stick_map, core_density):
     points = orbitals.shape[2] // 2
     rows_px, rows_py, groups = lax.axis_size("px"), lax.axis_size("py"), lax.axis_size("band")
-    px_index, py_index, band_index = lax.axis_index("px"), lax.axis_index("py"), lax.axis_index("band")
     dims = (points, rows_px, rows_py, groups)
     yblock = xblock = points // rows_px
-    zshare = points // (rows_py * groups)
     kyblock = points // (rows_py * groups)
-    density, mean = share_density(orbitals, occupations, stick_map, px_index)
-    core = lax.dynamic_slice_in_dim(core_density, band_index * zshare, zshare, 0)
-    shift = mean + CORE_TYPICAL
-    rho = density.transpose(1, 0, 2) + (core - shift)
-    rho = rho.reshape(zshare // 2, 2, yblock, points).transpose(1, 0, 2, 3).reshape(2, zshare // 2 * yblock, points)
-    _, freq = real_basis(points)
-    unit = 2.0 * math.pi / (points * SPACING)
-    all_q = (freq * freq).astype(np.float32)
-    lane_q = np.zeros((rows_px, LANES), np.float32)
-    lane_q[:, :xblock] = all_q.reshape(rows_px, xblock)
-    q_row = lax.dynamic_index_in_dim(jnp.asarray(lane_q), px_index, 0, keepdims=False)
-    q_col = lax.dynamic_slice_in_dim(jnp.asarray(all_q), (band_index * rows_py + py_index) * kyblock, kyblock)
-    squared = unit**2 * (q_col[:, None, None] + all_q[None, :, None] + q_row[None, None, :])
-    factor = jnp.where(squared > 0, 4.0 * math.pi / jnp.where(squared > 0, squared, 1.0), 0.0)
-    slope = lax.dynamic_index_in_dim(jnp.asarray(slope_tables(points, rows_py, groups)), py_index, 0, keepdims=False)
+    z_table, by_y, by_x = column_tables(points, rows_px, rows_py, groups)
+    sticks, places, notes = run_columns(occupations, orbitals, z_table, stick_map, dims)
+    rho, shift = run_density(notes, sticks, places, core_density, by_y, by_x, dims)
+    slope = jnp.asarray(slope_tables(points, rows_py, groups))
     tables = chain_tables(points, rows_px, rows_py, groups)
-    xs, gy, gz, h = run_chain(rho, factor, slope, tables, dims)
-    return tuple(run_final(xs, gy, gz, h, shift.reshape(1), points, yblock))
+    xs, gy, gz, h = run_chain(rho, slope, tables, dims)
+    return tuple(run_final(xs, gy, gz, h, shift, points, yblock))
 
 
 def body(orbitals, occupations, stick_map, core_density):
@@ -617,6 +821,7 @@
         share = points // (mesh.shape["py"] * mesh.shape["band"])
         fits = (
             points == LANES + HALF and block <= HALF and block % 16 == 0 and share % 8 == 0
+            and orbitals.shape[:2] == (1, LANES)
             and mesh.shape["py"] == 2 and mesh.shape["band"] == 4
         )
         return (fast_body if fits else body)(orbitals, occupations, stick_map, core_density)

time: 267 us -> 187 us (0.70)
  the two profiles are of different devices: /device:TPU:17 before, /device:TPU:1 now
where the time goes in v3:
time: 187 us; the launch traced here: 184 us
  Pallas kernels  177 us (95%)
  local copies, waits for them, and re-layouts  6.31 us (3%)
    pallas_call x1, Pallas kernels, run_chain(): pl.pallas_call(functools.partial(chain_kernel, dims), out_shape=[field] *...  111 us
    pallas_call x1, Pallas kernels, run_density(): pl.pallas_call(functools.partial(density_kernel, dims), out_shape=[jax.Sh...  24.1 us
    pallas_call x1, Pallas kernels, run_final(): pl.pallas_call(functools.partial(final_kernel, (points, yblock, pairs)),...  23.3 us
    pallas_call x1, Pallas kernels, run_columns(): pl.pallas_call(functools.partial(column_kernel, dims), out_shape=[jax.Sha...  18.9 us
    unnamed x14, local copies, waits for them, and re-layouts  6.31 us

profile of v3, /device:TPU:1, one launch (start us, length us, event | category | flops | bytes accessed | tf_op | source)
XLA Modules:
  0.0 184.5 jit_solution(18295665827292530648)
XLA Ops:
  1.3 18.9 %shard_map.176 = (bf16[4,8,48,128]{3,2,1,0:T(8,128)(2,1)}, s32[4,2,256]{2,1,0:T(2,128)}, f32[4,8,8,128]{3,2,1,0:T(8,128)}) custom-call(f32[1]{0:T(128)S(6)} %copy.19.occupation, bf16[1,128,384]{2,1,0:T(8,128)(2,1)} %orbitals.1, bf16[2,384,384]{2,1,0:T(8,128)(2,1)} %constant.26.clone.z_table, s32[2,256]{1,0:T(2,128)} %places.1), custom_call_target="tpu_custom_call" | custom-call | tf_op jit(solution)/shard_map/pallas_call | solution.py:610
  20.1 0.0 copy-start.1
  20.2 1.1 copy-done.1
  21.3 0.0 copy-start.2
  21.3 1.0 copy-done.2
  22.3 0.0 copy-start.3
  22.3 1.0 copy-done.3
  23.3 0.0 copy-start.4
  23.3 0.9 copy-done.4
  24.2 0.0 copy-start.5
  24.2 0.7 copy-done.5
  24.9 24.1 %shard_map.177 = (f32[2,576,192]{2,1,0:T(8,128)S(1)}, f32[8,128]{1,0:T(8,128)S(1)}) custom-call(f32[4,8,8,128]{3,2,1,0:T(8,128)S(1)} %copy-done.4, bf16[4,8,48,128]{3,2,1,0:T(8,128)(2,1)S(1)} %copy-done.3, s32[4,2,256]{2,1,0:T(2,128)S(1)} %copy-done.5, bf16[4,2,192,256]{3,2,1,0:T(8,128)(2,1)S(1)} %copy-done.1, bf16[2,2,192,192]{3,2,1,0:T(8,128)(2,1)S(1)} %copy-done.2, ...), custom_call_target="tpu_custom_call" | custom-call | tf_op jit(solution)/shard_map/pallas_call | solution.py:711
  49.0 0.0 copy-start
  49.0 1.0 copy-done
  50.0 0.0 copy-start.6
  50.0 0.6 copy-done.6
  50.6 110.5 %shard_map.178 = (bf16[4,576,384]{2,1,0:T(8,128)(2,1)}, bf16[4,576,384]{2,1,0:T(8,128)(2,1)}, bf16[4,576,384]{2,1,0:T(8,128)(2,1)}, bf16[4,576,384]{2,1,0:T(8,128)(2,1)}) custom-call(f32[2,576,192]{2,1,0:T(8,128)} %copy-done, bf16[2,2,192,896]{3,2,1,0:T(8,128)(2,1)} %constant.43.forward, bf16[384,192]{1,0:T(8,128)(2,1)} %constant.32.clone.y_in, ...), custom_call_target="tpu_custom_call" | custom-call | tf_op jit(solution)/shard_map/pallas_call | solution.py:450
  161.1 23.3 %shard_map.179 = (f32[96,48,192]{2,1,0:T(8,128)}, f32[3,96,48,192]{3,2,1,0:T(8,128)}) custom-call(f32[8,128]{1,0:T(8,128)} %copy-done.6, bf16[2304,384]{1,0:T(8,128)(2,1)} %bitcast.4, bf16[2304,384]{1,0:T(8,128)(2,1)} %bitcast.5, bf16[2304,384]{1,0:T(8,128)(2,1)} %bitcast.6, bf16[2304,384]{1,0:T(8,128)(2,1)} %bitcast.7, ...), custom_call_target="tpu_custom_call" | custom-call | tf_op jit(solution)/shard_map/pallas_call | solution.py:514
Async XLA Ops:
  20.1 1.1 copy-start.1
  21.3 1.0 copy-start.2
  22.3 1.0 copy-start.3
  23.3 0.9 copy-start.4
  24.2 0.7 copy-start.5
  49.0 1.0 copy-start
  50.0 0.6 copy-start.6

commit v4 on v3

--- a/solution.py
+++ b/solution.py
@@ -20,6 +20,9 @@
 HIGH = lax.Precision.HIGH
 CORE_LEAST = 0.05
 CORE_TYPICAL = 0.2
+PAIRS = 12
+COUNT = 24
+CHUNKS = 3
 
 
 def inverse_table(points):
@@ -211,9 +214,9 @@
 
 
 def chain_kernel(
-    dims, rho, forward, y_in, y_out, y_slope, z_in, z_out, spread, slope,
+    dims, summed, rho, forward, y_in, y_out, y_slope, z_in, z_out, spread, slope,
     xs, gy, gz, h,
-    others, c1s, c1, c2s, c2, c3s, c3, c4s, c4, gin, gs, wide, deep, sends, recvs,
+    others, c1s, c1, c2s, c2, c3s, c3, c4s, c4, gin, gs, wide, deep, sends, recvs, g_sends, g_recvs, b_sends, b_recvs,
 ):
     points, rows_px, rows_py, groups = dims
     yblock = points // rows_px
@@ -229,12 +232,6 @@
         (lax.rem(band + b, groups), lax.rem(py + q, rows_py))
         for b in range(groups) for q in range(rows_py) if b or q
     ]
-    barrier = pltpu.get_barrier_semaphore()
-    for peer in px_peers:
-        pl.semaphore_signal(barrier, inc=1, device_id=(band, peer, py), device_id_type=pl.DeviceIdType.MESH)
-    for peer_band, peer_py in zy_peers:
-        pl.semaphore_signal(barrier, inc=1, device_id=(peer_band, px, peer_py), device_id_type=pl.DeviceIdType.MESH)
-    pl.semaphore_wait(barrier, len(px_peers) + len(zy_peers))
     used = []
 
     def send(src, dst, device):
@@ -246,13 +243,13 @@
         copy.start()
         return copy
 
-    def to_px(src, dst):
-        return [send(src.at[peer], dst.at[px], (band, peer, py)) for peer in px_peers]
-
-    def to_zy(src, dst):
-        return [
-            send(src.at[b * rows_py + q], dst.at[me], (b, px, q)) for b, q in zy_peers
-        ]
+    def to_px(src, dst, cut):
+        dst[px, cut] = src[px, cut]
+        return [send(src.at[peer, cut], dst.at[px, cut], (band, peer, py)) for peer in px_peers]
+
+    def to_zy(src, dst, cut):
+        dst[me, cut] = src[me, cut]
+        return [send(src.at[b * rows_py + q, cut], dst.at[me, cut], (b, px, q)) for b, q in zy_peers]
 
     def arrived(copies):
         for copy in copies:
@@ -260,17 +257,21 @@
 
     right, left = lax.rem(band + 1, groups), lax.rem(band + groups - 1, groups)
 
-    def to_band(field, slot, target):
-        return send(field.at[slot], field.at[slot], (target, px, py))
+    def to_band(field, slot, target, cut=pl.ds(0, rows)):
+        return send(field.at[slot, cut], field.at[slot, cut], (target, px, py))
 
     def to_other(slot):
         return send(xs.at[slot], others.at[slot], (band, px, lax.rem(py + 1, rows_py)))
 
-    step = 2 * yblock
-
-    @pl.loop(0, rows // step)
-    def _(i):
-        at = pl.ds(pl.multiple_of(i * step, step), step)
+    step = zpairs // CHUNKS
+    lined = [pl.ds(c * step * yblock, step * yblock) for c in range(CHUNKS)]
+    short_cuts = [pl.ds(c * step * kyblock, step * kyblock) for c in range(CHUNKS)]
+    first, second, third, fourth, ring_right = [], [], [], [], []
+    h_right, h_left, h_far = [], [], []
+
+    def to_modes_x(c):
+        summed(c * step, (c + 1) * step)
+        at = lined[c]
         out = None
         for parity in range(2):
             high, low = split(rho[parity, at, :])
@@ -279,32 +280,82 @@
         xs[band, at, :] = out[:, : 3 * LANES].astype(BF)
         for p in range(rows_px):
             c1s[p, at, :] = out[:, (3 + p) * LANES : (4 + p) * LANES].astype(BF)
-
-    first = to_px(c1s, c1)
-    ring_right = to_band(xs, band, right)
+        first.append(to_px(c1s, c1, at))
+        ring_right.append(to_band(xs, band, right, at))
+
+    def to_modes_y(c):
+        arrived(first[c])
+
+        @pl.loop(c * step // 2, (c + 1) * step // 2)
+        def _(i):
+            found = []
+            for k in range(2):
+                at = pl.ds(pl.multiple_of((2 * i + k) * yblock, yblock), yblock)
+                out = dotf(y_in[...], jnp.concatenate([c1[p, at, :] for p in range(rows_px)], 0))
+                found.append(out[:points] + out[points:])
+            at = pl.ds(pl.multiple_of(i * 2 * kyblock, 2 * kyblock), 2 * kyblock)
+            for d in range(pieces):
+                cut = slice(d * kyblock, (d + 1) * kyblock)
+                c2s[d, at, :] = jnp.concatenate([f[cut] for f in found], 0).astype(BF)
+
+        second.append(to_zy(c2s, c2, short_cuts[c]))
+
+    for c in range(CHUNKS):
+        to_modes_x(c)
+        if c:
+            to_modes_y(c - 1)
+    to_modes_y(CHUNKS - 1)
+    far = lax.rem(band + 2, groups)
+    slots = [band, left, right, far]
     across = [to_other(band)]
-    c1[px] = c1s[px]
-    arrived(first)
-
-    @pl.loop(0, zpairs // 2)
-    def _(i):
-        found = []
-        for k in range(2):
-            at = pl.ds(pl.multiple_of((2 * i + k) * yblock, yblock), yblock)
-            out = dotf(y_in[...], jnp.concatenate([c1[p, at, :] for p in range(rows_px)], 0))
-            found.append(out[:points] + out[points:])
-        at = pl.ds(pl.multiple_of(i * 2 * kyblock, 2 * kyblock), 2 * kyblock)
-        for d in range(pieces):
-            cut = slice(d * kyblock, (d + 1) * kyblock)
-            c2s[d, at, :] = jnp.concatenate([f[cut] for f in found], 0).astype(BF)
-
-    second = to_zy(c2s, c2)
-    c2[me] = c2s[me]
+
+    def outward(k, source):
+        return pltpu.make_async_remote_copy(
+            src_ref=xs.at[slots[k]], dst_ref=gin.at[source], send_sem=g_sends.at[k], recv_sem=g_recvs.at[source],
+            device_id=(band, k, py), device_id_type=pl.DeviceIdType.MESH,
+        )
+
+    def spread_out(k):
+        @pl.when(px != k)
+        def _():
+            outward(k, px).start()
+
+        @pl.when(px == k)
+        def _():
+            gin[k] = xs[slots[k]]
+
+    def slot_of(p):
+        return jnp.where(p == 0, band, jnp.where(p == 1, left, jnp.where(p == 2, right, far)))
+
+    def homeward(k, peer, owner):
+        return pltpu.make_async_remote_copy(
+            src_ref=gs.at[peer], dst_ref=gy.at[slot_of(owner)], send_sem=b_sends.at[k], recv_sem=b_recvs.at[owner],
+            device_id=(band, peer, py), device_id_type=pl.DeviceIdType.MESH,
+        )
+
+    def slopes_along_y():
+        for peer in px_peers:
+            outward(0, peer).wait_recv()
+
+        @pl.loop(0, zpairs)
+        def _(i):
+            at = pl.ds(pl.multiple_of(i * yblock, yblock), yblock)
+            out = dotf(y_slope[...], jnp.concatenate([gin[p, at, :] for p in range(rows_px)], 0))
+            out = out[:points] + out[points:]
+            for p in range(rows_px):
+                gs[p, at, :] = out[p * yblock : (p + 1) * yblock].astype(BF)
+
+        for k, peer in enumerate(px_peers):
+            homeward(k, peer, px).start()
+        gy[slot_of(px)] = gs[px]
+
+    spread_out(0)
     ring_left = to_band(xs, band, left)
-    ring_right.wait_recv()
-    ring_far = to_band(xs, left, right)
+    arrived(ring_right)
     across.append(to_other(left))
-    arrived(second)
+    spread_out(1)
+    for copies in second:
+        arrived(copies)
     for d in range(pieces):
         wide[pl.ds(d * short, short), :] = c2[d].astype(F32)
     lane = lax.broadcasted_iota(jnp.int32, (points, 2 * LANES), 1) % LANES
@@ -341,59 +392,55 @@
 
     for d in range(pieces):
         c3s[d] = wide[pl.ds(d * short, short), :].astype(BF)
-    third = to_zy(c3s, c3)
-    c3[me] = c3s[me]
+    for c in range(CHUNKS):
+        third.append(to_zy(c3s, c3, short_cuts[c]))
+    ring_far = to_band(xs, left, right)
     ring_left.wait_recv()
     across.append(to_other(right))
-    ring_far.wait_recv()
-    far = lax.rem(band + 2, groups)
-    across.append(to_other(far))
-    outward = to_px(xs, gin)
-    gin[px] = xs[px]
-    arrived(third)
-    for d in range(pieces):
-        wide[pl.ds(d * short, short), :] = c3[d].astype(F32)
-
-    @pl.loop(0, zpairs)
-    def _(i):
-        data = jnp.concatenate(
-            [wide[pl.ds(pl.multiple_of(d * short + i * kyblock, 8), kyblock), :] for d in range(pieces)], 0
-        ).astype(BF)
-        out = dotf(y_out[...], data)
-        out = out[:points] + out[points:]
-        at = pl.ds(pl.multiple_of(i * yblock, yblock), yblock)
-        for p in range(rows_px):
-            c4s[p, at, :] = out[p * yblock : (p + 1) * yblock].astype(BF)
-
-    fourth = to_px(c4s, c4)
-    c4[px] = c4s[px]
-    arrived(fourth)
-
-    @pl.loop(0, rows // step)
-    def _(i):
-        at = pl.ds(pl.multiple_of(i * step, step), step)
+    spread_out(2)
+    pl.when(px < 2)(slopes_along_y)
+
+    def from_modes_y(c):
+        arrived(third[c])
+        for d in range(pieces):
+            wide[pl.ds(d * short + c * step * kyblock, step * kyblock), :] = c3[d, short_cuts[c], :].astype(F32)
+
+        @pl.loop(c * step, (c + 1) * step)
+        def _(i):
+            data = jnp.concatenate(
+                [wide[pl.ds(pl.multiple_of(d * short + i * kyblock, 8), kyblock), :] for d in range(pieces)], 0
+            ).astype(BF)
+            out = dotf(y_out[...], data)
+            out = out[:points] + out[points:]
+            at = pl.ds(pl.multiple_of(i * yblock, yblock), yblock)
+            for p in range(rows_px):
+                c4s[p, at, :] = out[p * yblock : (p + 1) * yblock].astype(BF)
+
+        fourth.append(to_px(c4s, c4, lined[c]))
+
+    def gathered_modes(c):
+        arrived(fourth[c])
+        at = lined[c]
         out = None
         for p in range(rows_px):
             part = dotf(c4[p, at, :], spread[p])
             out = part if out is None else out + part
         h[band, at, :] = out.astype(BF)
-
-    h_right = to_band(h, band, right)
-    h_left = to_band(h, band, left)
-    arrived(outward)
-
-    @pl.loop(0, zpairs)
-    def _(i):
-        at = pl.ds(pl.multiple_of(i * yblock, yblock), yblock)
-        out = dotf(y_slope[...], jnp.concatenate([gin[p, at, :] for p in range(rows_px)], 0))
-        out = out[:points] + out[points:]
-        for p in range(rows_px):
-            gs[p, at, :] = out[p * yblock : (p + 1) * yblock].astype(BF)
-
-    homeward = to_px(gs, gy)
-    gy[px] = gs[px]
-    h_right.wait_recv()
-    h_far = to_band(h, left, right)
+        h_right.append(to_band(h, band, right, at))
+        h_left.append(to_band(h, band, left, at))
+
+    for c in range(CHUNKS):
+        from_modes_y(c)
+        if c:
+            gathered_modes(c - 1)
+    gathered_modes(CHUNKS - 1)
+    ring_far.wait_recv()
+    across.append(to_other(far))
+    spread_out(3)
+    pl.when(px >= 2)(slopes_along_y)
+    for c in range(CHUNKS):
+        h_right[c].wait_recv()
+        h_far.append(to_band(h, left, right, lined[c]))
     arrived(across)
     own_rows = groups * rows
     for b in range(groups):
@@ -427,45 +474,15 @@
     for b in range(groups):
         for t in range(3):
             gz[b, :, pl.ds(t * LANES, LANES)] = deep[t, pl.ds(b * rows, rows), :].astype(BF)
-    h_left.wait_recv()
-    h_far.wait_recv()
-    arrived(homeward)
+    arrived(h_left)
+    arrived(h_far)
+    for k, peer in enumerate(px_peers):
+        homeward(k, px, peer).wait_recv()
+        homeward(k, peer, px).wait_send()
+    for k in range(rows_px):
+        pl.when(px != k)(outward(k, px).wait_send)
     for copy in used:
         copy.wait_send()
-
-
-def run_chain(rho, slope, tables, dims):
-    points, rows_px, rows_py, groups = dims
-    yblock = points // rows_px
-    zpairs = points // (rows_py * groups) // 2
-    pieces = groups * rows_py
-    kyblock = points // pieces
-    rows, short = zpairs * yblock, zpairs * kyblock
-    copies = 4 * (rows_px - 1) + 2 * (pieces - 1) + 3 + 3 + groups
-    field = jax.ShapeDtypeStruct((groups, rows, 3 * LANES), BF)
-    vmem = pl.BlockSpec(memory_space=pltpu.VMEM)
-    lined = pltpu.VMEM((rows_px, rows, LANES), BF)
-    cut = pltpu.VMEM((pieces, short, LANES), BF)
-    names = ("forward", "y_in", "y_out", "y_slope", "z_in", "z_out", "spread")
-    return pl.pallas_call(
-        functools.partial(chain_kernel, dims),
-        out_shape=[field] * 4,
-        in_specs=[vmem] * (len(names) + 2),
-        out_specs=[vmem] * 4,
-        scratch_shapes=[
-            pltpu.VMEM((groups, rows, 3 * LANES), BF),
-            lined, lined, cut, cut, cut, cut, lined, lined,
-            pltpu.VMEM((rows_px, rows, 3 * LANES), BF),
-            pltpu.VMEM((rows_px, rows, 3 * LANES), BF),
-            pltpu.VMEM((pieces * short, LANES), F32),
-            pltpu.VMEM((3, rows_py * groups * rows, LANES), F32),
-            pltpu.SemaphoreType.DMA((copies,)),
-            pltpu.SemaphoreType.DMA((copies,)),
-        ],
-        compiler_params=pltpu.CompilerParams(
-            collective_id=1, has_side_effects=True, vmem_limit_bytes=60 << 20
-        ),
-    )(rho, *[tables[n] for n in names], slope)
 
 
 def final_kernel(dims, shift, xs, gy, gz, h, table, potential, gradient):
@@ -488,13 +505,11 @@
         density, grad_y, grad_z, hartree = (out[k * n : (k + 1) * n] for k in range(4))
         density = jnp.maximum(density + shift[0:1, 0:1], CORE_LEAST)
         cube_root = jnp.exp(jnp.log(density) * (1.0 / 3.0))
-        four_thirds = density * cube_root
+        power = density * cube_root
+        power = power * power
         grad_square = grad_x * grad_x + grad_y * grad_y + grad_z * grad_z
-        scale = (PBE_MU / (PBE_KAPPA * REDUCED_SCALE)) * grad_square
-        inverse = 1.0 / (four_thirds * four_thirds + scale)
-        ratio = four_thirds * four_thirds * inverse
-        steep = scale * inverse
-        part = (4.0 / 3.0) * (1.0 + PBE_KAPPA - PBE_KAPPA * ratio) - (8.0 / 3.0) * PBE_KAPPA * steep * ratio
+        ratio = power / (power + (PBE_MU / (PBE_KAPPA * REDUCED_SCALE)) * grad_square)
+        part = 4.0 / 3.0 * (1.0 + PBE_KAPPA) - PBE_KAPPA * ratio * (4.0 - 8.0 / 3.0 * ratio)
         value = hartree - SLATER_COEF * cube_root * part
         for k in range(pairs):
             cut = slice(k * yblock, (k + 1) * yblock)
@@ -506,7 +521,7 @@
 
 def run_final(xs, gy, gz, h, shift, points, yblock):
     groups, rows, _ = xs.shape
-    pairs = 2
+    pairs = PAIRS
     steps = groups * rows // (pairs * yblock)
     zblock = steps * 2 * pairs
     table = final_tables(points)
@@ -538,7 +553,7 @@
     by_y = np.zeros((rows_px, 2, points, 2, HALF))
     by_y[:, :, :, :, :yblock] = inverse.reshape(2, points, 2, rows_px, yblock).transpose(3, 0, 1, 2, 4)
     by_y = np.concatenate([np.asarray(h) for h in two_halves(by_y.reshape(rows_px, 2, points, LANES))], 3)
-    by_x = np.stack([np.asarray(h) for h in two_halves(inverse[0].transpose(1, 2, 0))], 1)
+    by_x = np.concatenate([np.asarray(h) for h in two_halves(inverse[0].transpose(1, 2, 0).reshape(doubled, points))], 0)
     z_table = np.stack([np.asarray(h) for h in two_halves(z_order.reshape(doubled, doubled).T)])
     return jnp.asarray(z_table), jnp.asarray(by_y), jnp.asarray(by_x)
 
@@ -595,58 +610,30 @@
         send(middle, sticks.at[px], peer)
         send(notes.at[px], notes.at[px], peer)
     sticks[px] = middle[...]
-    for copy in used[first:]:
-        copy.wait_recv()
-    for copy in used:
-        copy.wait_send()
-
-
-def run_columns(occupations, orbitals, z_table, places, dims):
-    points, rows_px, rows_py, groups = dims
-    pieces = groups * rows_py
-    copies = 2 * (pieces - 1) + 3 * (rows_px - 1)
-    share = (pieces, 2 * points // pieces, LANES)
-    vmem = pl.BlockSpec(memory_space=pltpu.VMEM)
-    return pl.pallas_call(
-        functools.partial(column_kernel, dims),
-        out_shape=[
-            jax.ShapeDtypeStruct((rows_px,) + share, BF),
-            jax.ShapeDtypeStruct((rows_px,) + places.shape, jnp.int32),
-            jax.ShapeDtypeStruct((rows_px, pieces, 8, LANES), F32),
-        ],
-        in_specs=[pl.BlockSpec(memory_space=pltpu.SMEM)] + [vmem] * 3,
-        out_specs=[vmem] * 3,
-        scratch_shapes=[
-            pltpu.VMEM(share, BF),
-            pltpu.VMEM((8, LANES), F32),
-            pltpu.VMEM(share, BF),
-            pltpu.SemaphoreType.DMA((copies,)),
-            pltpu.SemaphoreType.DMA((copies,)),
-        ],
-        compiler_params=pltpu.CompilerParams(collective_id=2, has_side_effects=True),
-    )(occupations, orbitals, z_table, places)
-
-
-def density_kernel(dims, notes, sticks, places, by_y, by_x, core, rho, shift, wide, planes, held, sem):
+
+    def settled():
+        for copy in used[first:]:
+            copy.wait_recv()
+
+    def sent():
+        for copy in used:
+            copy.wait_send()
+
+    return settled, sent
+
+
+def density_kernel(dims, settled, notes, sticks, places, by_y, by_x, core, rho, shift, wide, planes, held, sem):
     points, rows_px, rows_py, groups = dims
     xblock = yblock = points // rows_px
     zshare = points // (rows_py * groups)
     band, px = lax.axis_index("band"), lax.axis_index("px")
     fetch = pltpu.make_async_copy(core.at[pl.ds(band * zshare, zshare)], held, sem)
     fetch.start()
-    mean = CORE_TYPICAL
-    for p in range(rows_px):
-        for d in range(groups * rows_py):
-            mean = mean + notes[p, d, :, 1:2]
-    shift[...] = jnp.broadcast_to(mean, (8, LANES))
-    mean = mean[0:1]
-    weights = [notes[0, b * rows_py, 0:1, 0:1] for b in range(groups)]
-    count = 8
+    count = COUNT
     lines = groups * zshare
     sticks_px = rows_py * LANES
 
-    @pl.loop(0, rows_px)
-    def _(p):
+    def spread_along_y(p):
         wide[...] = sticks[p].astype(F32)
         spots = places[p]
         at_y = lax.broadcasted_iota(jnp.int32, (points, sticks_px), 0) == spots[1:2, :]
@@ -680,64 +667,137 @@
                     k * xblock : (k + 1) * xblock
                 ]
 
+    spread_along_y(px)
+    settled()
+
+    @pl.loop(1, rows_px)
+    def _(s):
+        spread_along_y(lax.rem(px + s, rows_px))
+
+    mean = CORE_TYPICAL
+    for p in range(rows_px):
+        for d in range(groups * rows_py):
+            mean = mean + notes[p, d, :, 1:2]
+    shift[...] = jnp.broadcast_to(mean, (8, LANES))
+    mean = mean[0:1]
+    weights = [notes[0, b * rows_py, 0:1, 0:1] for b in range(groups)]
     fetch.wait()
     lane = lax.broadcasted_iota(jnp.int32, (points, LANES), 1)
     sign = jnp.where(lane < HALF, -1.0, 1.0)
 
-    @pl.loop(0, zshare // 2)
-    def _(i):
-        total = [None, None]
-        for b in range(groups):
-            both = jnp.concatenate([planes[b * zshare + 2 * i + k] for k in range(2)], 1)
-            cosine = dotf(by_x[0, 0], both) + dotf(by_x[0, 1], both)
-            sine = dotf(by_x[1, 0], both) + dotf(by_x[1, 1], both)
+    def summed(start, stop):
+        @pl.loop(start, stop)
+        def _(i):
+            total = [None, None]
+            for b in range(groups):
+                both = jnp.concatenate([planes[b * zshare + 2 * i + k] for k in range(2)], 1)
+                out = dotf(by_x[...], both)
+                out = out[: 2 * points] + out[2 * points :]
+                cosine, sine = out[:points], out[points:]
+                for k in range(2):
+                    cut = slice(k * LANES, (k + 1) * LANES)
+                    value = cosine[:, cut] + sign * pltpu.roll(sine[:, cut], HALF, 1)
+                    value = weights[b] * (value * value)
+                    total[k] = value if b == 0 else total[k] + value
             for k in range(2):
-                cut = slice(k * LANES, (k + 1) * LANES)
-                value = cosine[:, cut] + sign * pltpu.roll(sine[:, cut], HALF, 1)
-                value = weights[b] * (value * value)
-                total[k] = value if b == 0 else total[k] + value
-        for k in range(2):
-            density = total[k] + pltpu.roll(total[k], HALF, 1)
-            rho[k, pl.ds(pl.multiple_of(i * yblock, yblock), yblock), :] = (
-                density.T[:yblock] + (held[2 * i + k] - mean)
-            )
-
-
-def run_density(notes, sticks, places, core, by_y, by_x, dims):
+                density = total[k] + pltpu.roll(total[k], HALF, 1)
+                rho[k, pl.ds(pl.multiple_of(i * yblock, yblock), yblock), :] = (
+                    density.T[:yblock] + (held[2 * i + k] - mean)
+                )
+
+    return summed
+
+
+COLUMN_INPUTS, DENSITY_INPUTS, CHAIN_INPUTS = 4, 3, 8
+
+
+def whole_kernel(dims, counts, *refs):
+    groups = [COLUMN_INPUTS, DENSITY_INPUTS, CHAIN_INPUTS, 5] + counts
+    parts, at = [], 0
+    for count in groups:
+        parts.append(refs[at : at + count])
+        at += count
+    column_in, density_in, chain_in, out, shared, column_own, density_own, chain_own = parts
+    sticks, places, notes, rho = shared
+    fields, shift = out[:4], out[4]
+    settled, sent = column_kernel(dims, *column_in, sticks, places, notes, *column_own)
+    summed = density_kernel(dims, settled, notes, sticks, places, *density_in, rho, shift, *density_own)
+    chain_kernel(dims, summed, rho, *chain_in, *fields, *chain_own)
+    sent()
+
+
+def run_whole(occupations, orbitals, stick_map, core, dims):
     points, rows_px, rows_py, groups = dims
-    zshare = points // (rows_py * groups)
-    yblock = points // rows_px
+    xblock = yblock = points // rows_px
+    pieces = groups * rows_py
+    kyblock = zshare = points // pieces
+    zpairs = zshare // 2
+    rows, short = zpairs * yblock, zpairs * kyblock
+    z_table, by_y, by_x = column_tables(points, rows_px, rows_py, groups)
+    tables = chain_tables(points, rows_px, rows_py, groups)
+    names = ("forward", "y_in", "y_out", "y_slope", "z_in", "z_out", "spread")
+    slope = jnp.asarray(slope_tables(points, rows_py, groups))
+    share = (pieces, 2 * zshare, LANES)
+    field = jax.ShapeDtypeStruct((groups, rows, 3 * LANES), BF)
     vmem = pl.BlockSpec(memory_space=pltpu.VMEM)
+    lined = pltpu.VMEM((rows_px, rows, LANES), BF)
+    cut = pltpu.VMEM((pieces, short, LANES), BF)
+    dma = pltpu.SemaphoreType.DMA
+    column_copies = 2 * (pieces - 1) + 3 * (rows_px - 1)
+    chain_copies = CHUNKS * (2 * (rows_px - 1) + 2 * (pieces - 1) + 1 + 3) + 2 + groups
+    shared = [
+        pltpu.VMEM((rows_px,) + share, BF),
+        pltpu.VMEM((rows_px,) + stick_map.shape, jnp.int32),
+        pltpu.VMEM((rows_px, pieces, 8, LANES), F32),
+        pltpu.VMEM((2, rows, points), F32),
+    ]
+    column_own = [
+        pltpu.VMEM(share, BF),
+        pltpu.VMEM((8, LANES), F32),
+        pltpu.VMEM(share, BF),
+        dma((column_copies,)),
+        dma((column_copies,)),
+    ]
+    density_own = [
+        pltpu.VMEM(share, F32),
+        pltpu.VMEM((groups * zshare, points, LANES), BF),
+        pltpu.VMEM((zshare, yblock, points), F32),
+        dma,
+    ]
+    chain_own = [
+        pltpu.VMEM((groups, rows, 3 * LANES), BF),
+        lined, lined, cut, cut, cut, cut, lined, lined,
+        pltpu.VMEM((rows_px, rows, 3 * LANES), BF),
+        pltpu.VMEM((rows_px, rows, 3 * LANES), BF),
+        pltpu.VMEM((pieces * short, LANES), F32),
+        pltpu.VMEM((3, rows_py * groups * rows, LANES), F32),
+        dma((chain_copies,)),
+        dma((chain_copies,)),
+        dma((rows_px,)),
+        dma((rows_px,)),
+        dma((rows_px - 1,)),
+        dma((rows_px,)),
+    ]
+    counts = [len(part) for part in (shared, column_own, density_own, chain_own)]
     return pl.pallas_call(
-        functools.partial(density_kernel, dims),
-        out_shape=[
-            jax.ShapeDtypeStruct((2, zshare // 2 * yblock, points), F32),
-            jax.ShapeDtypeStruct((8, LANES), F32),
-        ],
-        in_specs=[vmem] * 5 + [pl.BlockSpec(memory_space=pl.ANY)],
-        out_specs=[vmem] * 2,
-        scratch_shapes=[
-            pltpu.VMEM(sticks.shape[1:], F32),
-            pltpu.VMEM((groups * zshare, points, LANES), BF),
-            pltpu.VMEM((zshare, yblock, points), F32),
-            pltpu.SemaphoreType.DMA,
-        ],
-        compiler_params=pltpu.CompilerParams(vmem_limit_bytes=48 << 20),
-    )(notes, sticks, places, by_y, by_x, core)
+        functools.partial(whole_kernel, dims, counts),
+        out_shape=[field] * 4 + [jax.ShapeDtypeStruct((8, LANES), F32)],
+        in_specs=[pl.BlockSpec(memory_space=pltpu.SMEM)]
+        + [vmem] * 5
+        + [pl.BlockSpec(memory_space=pl.ANY)]
+        + [vmem] * 8,
+        out_specs=[vmem] * 5,
+        scratch_shapes=shared + column_own + density_own + chain_own,
+        compiler_params=pltpu.CompilerParams(collective_id=1, has_side_effects=True, vmem_limit_bytes=60 << 20),
+    )(occupations, orbitals, z_table, stick_map, by_y, by_x, core, *[tables[n] for n in names], slope)
 
 
 def fast_body(orbitals, occupations, stick_map, core_density):
     points = orbitals.shape[2] // 2
     rows_px, rows_py, groups = lax.axis_size("px"), lax.axis_size("py"), lax.axis_size("band")
     dims = (points, rows_px, rows_py, groups)
-    yblock = xblock = points // rows_px
-    kyblock = points // (rows_py * groups)
-    z_table, by_y, by_x = column_tables(points, rows_px, rows_py, groups)
-    sticks, places, notes = run_columns(occupations, orbitals, z_table, stick_map, dims)
-    rho, shift = run_density(notes, sticks, places, core_density, by_y, by_x, dims)
-    slope = jnp.asarray(slope_tables(points, rows_py, groups))
-    tables = chain_tables(points, rows_px, rows_py, groups)
-    xs, gy, gz, h = run_chain(rho, slope, tables, dims)
+    yblock = points // rows_px
+    xs, gy, gz, h, shift = run_whole(occupations, orbitals, stick_map, core_density, dims)
     return tuple(run_final(xs, gy, gz, h, shift, points, yblock))
 
 
@@ -822,7 +882,7 @@
         fits = (
             points == LANES + HALF and block <= HALF and block % 16 == 0 and share % 8 == 0
             and orbitals.shape[:2] == (1, LANES)
-            and mesh.shape["py"] == 2 and mesh.shape["band"] == 4
+            and mesh.shape["py"] == 2 and mesh.shape["band"] == 4 and mesh.shape["px"] == 4
         )
         return (fast_body if fits else body)(orbitals, occupations, stick_map, core_density)
 

time: 187 us -> 155 us (0.83)
  the two profiles are of different devices: /device:TPU:1 before, /device:TPU:3 now
where the time goes in v4:
time: 155 us
  Pallas kernels  154 us (99%)
    pallas_call x1, Pallas kernels, run_whole(): pl.pallas_call(functools.partial(whole_kernel, dims, counts), out_shape=[...  140 us
    pallas_call x1, Pallas kernels, run_final(): pl.pallas_call(functools.partial(final_kernel, (points, yblock, pairs)),...  14 us

profile of v4, /device:TPU:3, one launch (start us, length us, event | category | flops | bytes accessed | tf_op | source)
XLA Modules:
  0.0 155.0 jit_solution(9793847133578199990)
XLA Ops:
  1.3 139.7 %shard_map.176 = (bf16[4,576,384]{2,1,0:T(8,128)(2,1)}, bf16[4,576,384]{2,1,0:T(8,128)(2,1)}, bf16[4,576,384]{2,1,0:T(8,128)(2,1)}, bf16[4,576,384]{2,1,0:T(8,128)(2,1)}, f32[8,128]{1,0:T(8,128)}) custom-call(f32[1]{0:T(128)S(6)} %copy.19.refs_0_, bf16[1,128,384]{2,1,0:T(8,128)(2,1)} %refs_1_.1, bf16[2,384,384]{2,1,0:T(8,128)(2,1)} %constant.26.clone.refs_2_, ...), custom_call_target="tpu_custom_call" | custom-call | tf_op jit(solution)/shard_map/pallas_call | solution.py:782
  141.0 14.0 %shard_map.177 = (f32[96,48,192]{2,1,0:T(8,128)}, f32[3,96,48,192]{3,2,1,0:T(8,128)}) custom-call(f32[8,128]{1,0:T(8,128)} %get-tuple-element.7.shift, bf16[2304,384]{1,0:T(8,128)(2,1)} %bitcast.4, bf16[2304,384]{1,0:T(8,128)(2,1)} %bitcast.5, bf16[2304,384]{1,0:T(8,128)(2,1)} %bitcast.6, bf16[2304,384]{1,0:T(8,128)(2,1)} %bitcast.7, ...), custom_call_target="tpu_custom_call" | custom-call | tf_op jit(solution)/shard_map/pallas_call | solution.py:529

commit v5 on v4

--- a/solution.py
+++ b/solution.py
@@ -217,6 +217,7 @@
     dims, summed, rho, forward, y_in, y_out, y_slope, z_in, z_out, spread, slope,
     xs, gy, gz, h,
     others, c1s, c1, c2s, c2, c3s, c3, c4s, c4, gin, gs, wide, deep, sends, recvs, g_sends, g_recvs, b_sends, b_recvs,
+    o_sends, o_recvs, x_sends, x_recvs, h_sends, h_recvs,
 ):
     points, rows_px, rows_py, groups = dims
     yblock = points // rows_px
@@ -255,19 +256,49 @@
         for copy in copies:
             copy.wait_recv()
 
-    right, left = lax.rem(band + 1, groups), lax.rem(band + groups - 1, groups)
-
-    def to_band(field, slot, target, cut=pl.ds(0, rows)):
-        return send(field.at[slot, cut], field.at[slot, cut], (target, px, py))
+    def hop(field, out_sems, in_sems, sign, phase, c):
+        slot = jnp.clip(band - sign * phase, 0, groups - 1)
+        target = jnp.clip(band + sign, 0, groups - 1)
+        return pltpu.make_async_remote_copy(
+            src_ref=field.at[slot, lined[c]], dst_ref=field.at[slot, lined[c]],
+            send_sem=out_sems.at[phase * 2 + (sign > 0), c], recv_sem=in_sems.at[slot, c],
+            device_id=(target, px, py), device_id_type=pl.DeviceIdType.MESH,
+        )
+
+    def hops(phase):
+        return [
+            (1, (band >= phase) & (band < groups - 1)),
+            (-1, (band + phase < groups) & (band > 0)),
+        ]
+
+    def launch(fields, phase, c):
+        for sign, runs in hops(phase):
+            pl.when(runs)(hop(*fields, sign, phase, c).start)
+
+    def landed(fields, distance, c):
+        for sign in (1, -1):
+            slot = band - sign * distance
+
+            @pl.when((slot >= 0) & (slot < groups))
+            def _():
+                pltpu.make_async_remote_copy(
+                    src_ref=fields[0].at[0, lined[c]], dst_ref=fields[0].at[jnp.clip(slot, 0, groups - 1), lined[c]],
+                    send_sem=fields[1].at[0, c], recv_sem=fields[2].at[jnp.clip(slot, 0, groups - 1), c],
+                    device_id=(band, px, py), device_id_type=pl.DeviceIdType.MESH,
+                ).wait_recv()
 
     def to_other(slot):
-        return send(xs.at[slot], others.at[slot], (band, px, lax.rem(py + 1, rows_py)))
-
+        return pltpu.make_async_remote_copy(
+            src_ref=xs.at[slot], dst_ref=others.at[slot], send_sem=o_sends.at[slot], recv_sem=o_recvs.at[slot],
+            device_id=(band, px, lax.rem(py + 1, rows_py)), device_id_type=pl.DeviceIdType.MESH,
+        )
+
+    x_line = (xs, x_sends, x_recvs)
+    h_line = (h, h_sends, h_recvs)
     step = zpairs // CHUNKS
     lined = [pl.ds(c * step * yblock, step * yblock) for c in range(CHUNKS)]
     short_cuts = [pl.ds(c * step * kyblock, step * kyblock) for c in range(CHUNKS)]
-    first, second, third, fourth, ring_right = [], [], [], [], []
-    h_right, h_left, h_far = [], [], []
+    first, second, third, fourth = [], [], [], []
 
     def to_modes_x(c):
         summed(c * step, (c + 1) * step)
@@ -281,7 +312,7 @@
         for p in range(rows_px):
             c1s[p, at, :] = out[:, (3 + p) * LANES : (4 + p) * LANES].astype(BF)
         first.append(to_px(c1s, c1, at))
-        ring_right.append(to_band(xs, band, right, at))
+        launch(x_line, 0, c)
 
     def to_modes_y(c):
         arrived(first[c])
@@ -305,55 +336,60 @@
         if c:
             to_modes_y(c - 1)
     to_modes_y(CHUNKS - 1)
-    far = lax.rem(band + 2, groups)
-    slots = [band, left, right, far]
-    across = [to_other(band)]
-
-    def outward(k, source):
+
+    def outward(slot, source, c):
         return pltpu.make_async_remote_copy(
-            src_ref=xs.at[slots[k]], dst_ref=gin.at[source], send_sem=g_sends.at[k], recv_sem=g_recvs.at[source],
-            device_id=(band, k, py), device_id_type=pl.DeviceIdType.MESH,
+            src_ref=xs.at[slot, lined[c]], dst_ref=gin.at[source, lined[c]],
+            send_sem=g_sends.at[slot, c], recv_sem=g_recvs.at[source, c],
+            device_id=(band, slot, py), device_id_type=pl.DeviceIdType.MESH,
         )
 
-    def spread_out(k):
-        @pl.when(px != k)
+    def pass_on(slot, c):
+        pl.when(px != slot)(lambda: outward(slot, px, c).start())
+
+        @pl.when(px == slot)
         def _():
-            outward(k, px).start()
-
-        @pl.when(px == k)
-        def _():
-            gin[k] = xs[slots[k]]
-
-    def slot_of(p):
-        return jnp.where(p == 0, band, jnp.where(p == 1, left, jnp.where(p == 2, right, far)))
-
-    def homeward(k, peer, owner):
+            gin[px, lined[c]] = xs[slot, lined[c]]
+
+    def at_distance(distance, act):
+        for sign in (1, -1):
+            slot = band - sign * distance
+            pl.when((slot >= 0) & (slot < groups))(lambda: act(jnp.clip(slot, 0, groups - 1)))
+
+    def cross_over(slot):
+        to_other(slot).start()
+
+    def homeward(k, peer, owner, c):
         return pltpu.make_async_remote_copy(
-            src_ref=gs.at[peer], dst_ref=gy.at[slot_of(owner)], send_sem=b_sends.at[k], recv_sem=b_recvs.at[owner],
+            src_ref=gs.at[peer, lined[c]], dst_ref=gy.at[owner, lined[c]],
+            send_sem=b_sends.at[k, c], recv_sem=b_recvs.at[owner, c],
             device_id=(band, peer, py), device_id_type=pl.DeviceIdType.MESH,
         )
 
     def slopes_along_y():
-        for peer in px_peers:
-            outward(0, peer).wait_recv()
-
-        @pl.loop(0, zpairs)
-        def _(i):
-            at = pl.ds(pl.multiple_of(i * yblock, yblock), yblock)
-            out = dotf(y_slope[...], jnp.concatenate([gin[p, at, :] for p in range(rows_px)], 0))
-            out = out[:points] + out[points:]
-            for p in range(rows_px):
-                gs[p, at, :] = out[p * yblock : (p + 1) * yblock].astype(BF)
-
-        for k, peer in enumerate(px_peers):
-            homeward(k, peer, px).start()
-        gy[slot_of(px)] = gs[px]
-
-    spread_out(0)
-    ring_left = to_band(xs, band, left)
-    arrived(ring_right)
-    across.append(to_other(left))
-    spread_out(1)
+        for c in range(CHUNKS):
+            for peer in px_peers:
+                outward(0, peer, c).wait_recv()
+
+            @pl.loop(c * step, (c + 1) * step)
+            def _(i):
+                at = pl.ds(pl.multiple_of(i * yblock, yblock), yblock)
+                out = dotf(y_slope[...], jnp.concatenate([gin[p, at, :] for p in range(rows_px)], 0))
+                out = out[:points] + out[points:]
+                for p in range(rows_px):
+                    gs[p, at, :] = out[p * yblock : (p + 1) * yblock].astype(BF)
+
+            for k, peer in enumerate(px_peers):
+                homeward(k, peer, px, c).start()
+            gy[px, lined[c]] = gs[px, lined[c]]
+
+    near = (px - band <= 1) & (band - px <= 1)
+    for c in range(CHUNKS):
+        pass_on(band, c)
+    for c in range(CHUNKS):
+        landed(x_line, 1, c)
+        launch(x_line, 1, c)
+        at_distance(1, functools.partial(pass_on, c=c))
     for copies in second:
         arrived(copies)
     for d in range(pieces):
@@ -394,11 +430,14 @@
         c3s[d] = wide[pl.ds(d * short, short), :].astype(BF)
     for c in range(CHUNKS):
         third.append(to_zy(c3s, c3, short_cuts[c]))
-    ring_far = to_band(xs, left, right)
-    ring_left.wait_recv()
-    across.append(to_other(right))
-    spread_out(2)
-    pl.when(px < 2)(slopes_along_y)
+    for c in range(CHUNKS):
+        landed(x_line, 2, c)
+        launch(x_line, 2, c)
+        at_distance(2, functools.partial(pass_on, c=c))
+    cross_over(band)
+    at_distance(1, cross_over)
+    at_distance(2, cross_over)
+    pl.when(near)(slopes_along_y)
 
     def from_modes_y(c):
         arrived(third[c])
@@ -426,22 +465,26 @@
             part = dotf(c4[p, at, :], spread[p])
             out = part if out is None else out + part
         h[band, at, :] = out.astype(BF)
-        h_right.append(to_band(h, band, right, at))
-        h_left.append(to_band(h, band, left, at))
+        launch(h_line, 0, c)
 
     for c in range(CHUNKS):
         from_modes_y(c)
         if c:
             gathered_modes(c - 1)
     gathered_modes(CHUNKS - 1)
-    ring_far.wait_recv()
-    across.append(to_other(far))
-    spread_out(3)
-    pl.when(px >= 2)(slopes_along_y)
     for c in range(CHUNKS):
-        h_right[c].wait_recv()
-        h_far.append(to_band(h, left, right, lined[c]))
-    arrived(across)
+        landed(h_line, 1, c)
+        launch(h_line, 1, c)
+    for c in range(CHUNKS):
+        landed(x_line, 3, c)
+        at_distance(3, functools.partial(pass_on, c=c))
+    at_distance(3, cross_over)
+    pl.when(jnp.logical_not(near))(slopes_along_y)
+    for c in range(CHUNKS):
+        landed(h_line, 2, c)
+        launch(h_line, 2, c)
+    for slot in range(groups):
+        to_other(slot).wait_recv()
     own_rows = groups * rows
     for b in range(groups):
         for t in range(3):
@@ -474,13 +517,21 @@
     for b in range(groups):
         for t in range(3):
             gz[b, :, pl.ds(t * LANES, LANES)] = deep[t, pl.ds(b * rows, rows), :].astype(BF)
-    arrived(h_left)
-    arrived(h_far)
+    for c in range(CHUNKS):
+        landed(h_line, 3, c)
     for k, peer in enumerate(px_peers):
-        homeward(k, px, peer).wait_recv()
-        homeward(k, peer, px).wait_send()
-    for k in range(rows_px):
-        pl.when(px != k)(outward(k, px).wait_send)
+        for c in range(CHUNKS):
+            homeward(k, px, peer, c).wait_recv()
+            homeward(k, peer, px, c).wait_send()
+    for slot in range(groups):
+        to_other(slot).wait_send()
+        for c in range(CHUNKS):
+            pl.when(px != slot)(outward(slot, px, c).wait_send)
+    for line in (x_line, h_line):
+        for phase in range(groups - 1):
+            for sign, runs in hops(phase):
+                for c in range(CHUNKS):
+                    pl.when(runs)(hop(*line, sign, phase, c).wait_send)
     for copy in used:
         copy.wait_send()
 
@@ -744,7 +795,7 @@
     cut = pltpu.VMEM((pieces, short, LANES), BF)
     dma = pltpu.SemaphoreType.DMA
     column_copies = 2 * (pieces - 1) + 3 * (rows_px - 1)
-    chain_copies = CHUNKS * (2 * (rows_px - 1) + 2 * (pieces - 1) + 1 + 3) + 2 + groups
+    chain_copies = CHUNKS * (2 * (rows_px - 1) + 2 * (pieces - 1))
     shared = [
         pltpu.VMEM((rows_px,) + share, BF),
         pltpu.VMEM((rows_px,) + stick_map.shape, jnp.int32),
@@ -773,11 +824,13 @@
         pltpu.VMEM((3, rows_py * groups * rows, LANES), F32),
         dma((chain_copies,)),
         dma((chain_copies,)),
-        dma((rows_px,)),
-        dma((rows_px,)),
-        dma((rows_px - 1,)),
-        dma((rows_px,)),
-    ]
+        dma((rows_px, CHUNKS)),
+        dma((rows_px, CHUNKS)),
+        dma((rows_px - 1, CHUNKS)),
+        dma((rows_px, CHUNKS)),
+        dma((groups,)),
+        dma((groups,)),
+    ] + [dma((2 * (groups - 1), CHUNKS)), dma((groups, CHUNKS))] * 2
     counts = [len(part) for part in (shared, column_own, density_own, chain_own)]
     return pl.pallas_call(
         functools.partial(whole_kernel, dims, counts),

time: 155 us -> 150 us (0.968)
  the two profiles are of different devices: /device:TPU:3 before, /device:TPU:1 now
where the time goes in v5:
time: 150 us; the launch traced here: 149 us
  Pallas kernels  148 us (99%)
    pallas_call x1, Pallas kernels, run_whole(): pl.pallas_call(functools.partial(whole_kernel, dims, counts), out_shape=[...  134 us
    pallas_call x1, Pallas kernels, run_final(): pl.pallas_call(functools.partial(final_kernel, (points, yblock, pairs)),...  14 us

profile of v5, /device:TPU:1, one launch (start us, length us, event | category | flops | bytes accessed | tf_op | source)
XLA Modules:
  0.0 149.3 jit_solution(15046975810264211525)
XLA Ops:
  1.3 134.1 %shard_map.176 = (bf16[4,576,384]{2,1,0:T(8,128)(2,1)}, bf16[4,576,384]{2,1,0:T(8,128)(2,1)}, bf16[4,576,384]{2,1,0:T(8,128)(2,1)}, bf16[4,576,384]{2,1,0:T(8,128)(2,1)}, f32[8,128]{1,0:T(8,128)}) custom-call(f32[1]{0:T(128)S(6)} %copy.19.refs_0_, bf16[1,128,384]{2,1,0:T(8,128)(2,1)} %refs_1_.1, bf16[2,384,384]{2,1,0:T(8,128)(2,1)} %constant.26.clone.refs_2_, ...), custom_call_target="tpu_custom_call" | custom-call | tf_op jit(solution)/shard_map/pallas_call | solution.py:835
  135.4 14.0 %shard_map.177 = (f32[96,48,192]{2,1,0:T(8,128)}, f32[3,96,48,192]{3,2,1,0:T(8,128)}) custom-call(f32[8,128]{1,0:T(8,128)} %get-tuple-element.7.shift, bf16[2304,384]{1,0:T(8,128)(2,1)} %bitcast.4, bf16[2304,384]{1,0:T(8,128)(2,1)} %bitcast.5, bf16[2304,384]{1,0:T(8,128)(2,1)} %bitcast.6, bf16[2304,384]{1,0:T(8,128)(2,1)} %bitcast.7, ...), custom_call_target="tpu_custom_call" | custom-call | tf_op jit(solution)/shard_map/pallas_call | solution.py:580

commit v6 on v5

--- a/solution.py
+++ b/solution.py
@@ -429,11 +429,11 @@
     for d in range(pieces):
         c3s[d] = wide[pl.ds(d * short, short), :].astype(BF)
     for c in range(CHUNKS):
-        third.append(to_zy(c3s, c3, short_cuts[c]))
-    for c in range(CHUNKS):
         landed(x_line, 2, c)
         launch(x_line, 2, c)
         at_distance(2, functools.partial(pass_on, c=c))
+    for c in range(CHUNKS):
+        third.append(to_zy(c3s, c3, short_cuts[c]))
     cross_over(band)
     at_distance(1, cross_over)
     at_distance(2, cross_over)

time: 150 us -> 149 us (level)
  no operation moved by 1% of the time
where the time goes in v6:
time: 149 us
  Pallas kernels  148 us (99%)
    pallas_call x1, Pallas kernels, run_whole(): pl.pallas_call(functools.partial(whole_kernel, dims, counts), out_shape=[...  134 us
    pallas_call x1, Pallas kernels, run_final(): pl.pallas_call(functools.partial(final_kernel, (points, yblock, pairs)),...  14 us

profile of v6, /device:TPU:1, one launch (start us, length us, event | category | flops | bytes accessed | tf_op | source)
XLA Modules:
  0.0 149.2 jit_solution(366695280562869050)
XLA Ops:
  1.3 134.0 %shard_map.176 = (bf16[4,576,384]{2,1,0:T(8,128)(2,1)}, bf16[4,576,384]{2,1,0:T(8,128)(2,1)}, bf16[4,576,384]{2,1,0:T(8,128)(2,1)}, bf16[4,576,384]{2,1,0:T(8,128)(2,1)}, f32[8,128]{1,0:T(8,128)}) custom-call(f32[1]{0:T(128)S(6)} %copy.19.refs_0_, bf16[1,128,384]{2,1,0:T(8,128)(2,1)} %refs_1_.1, bf16[2,384,384]{2,1,0:T(8,128)(2,1)} %constant.26.clone.refs_2_, ...), custom_call_target="tpu_custom_call" | custom-call | tf_op jit(solution)/shard_map/pallas_call | solution.py:835
  135.2 14.0 %shard_map.177 = (f32[96,48,192]{2,1,0:T(8,128)}, f32[3,96,48,192]{3,2,1,0:T(8,128)}) custom-call(f32[8,128]{1,0:T(8,128)} %get-tuple-element.7.shift, bf16[2304,384]{1,0:T(8,128)(2,1)} %bitcast.4, bf16[2304,384]{1,0:T(8,128)(2,1)} %bitcast.5, bf16[2304,384]{1,0:T(8,128)(2,1)} %bitcast.6, bf16[2304,384]{1,0:T(8,128)(2,1)} %bitcast.7, ...), custom_call_target="tpu_custom_call" | custom-call | tf_op jit(solution)/shard_map/pallas_call | solution.py:580
